TPU v7x, 128 devices: a whole 4x4x4 slice. The times are simulated.
128 devices in a mesh: seq: 32 (over z, y, x_lo), tp: 2 (over core), pp: 2 (over x_hi).
Axes of the slice: x: 4 (x_hi: 2, x_lo: 2; x = x_hi * 2 + x_lo), y: 4, z: 4, core: 2. Of those that a mesh axis runs over, the one named last changes fastest.
Arguments:
- queries: bfloat16 [2, 16384, 4096], P('pp', 'seq', 'tp'), may hold values from -1.796875 to 1.796875
- keys: bfloat16 [2, 16384, 4096], P('pp', 'seq', 'tp'), may hold values from -1.796875 to 1.796875
- values: bfloat16 [2, 16384, 4096], P('pp', 'seq', 'tp'), may hold values from -25.375 to 25.375
- upstream: bfloat16 [2, 16384, 3072], P('pp', 'seq', 'tp'), may hold values from -6 to 6
- out_weight: bfloat16 [2, 4096, 3072], P('pp', 'tp'), may hold values from -0.09375 to 0.09375
- gain: float32 [2, 4096], P('pp', 'tp'), may hold values from 0.25 to 1.75
- log_decay: float32 [2, 32, 16384], P('pp', 'tp', 'seq'), may hold values from -0.7 to 0
Outputs:
- grad_queries: bfloat16 [2, 16384, 4096], P('pp', 'seq', 'tp')
- grad_keys: bfloat16 [2, 16384, 4096], P('pp', 'seq', 'tp')
- grad_values: bfloat16 [2, 16384, 4096], P('pp', 'seq', 'tp')
All inputs are finite; a program needn't handle non-finite values.
Results may differ from a plain program's by a relative error of at most 0.014.
Values may be sent and summed in bfloat16 or wider, within the bound.
A program may use at most 128 MiB of HBM per device.

v0:
```python
import jax
import jax.numpy as jnp
from jax import lax
from jax.sharding import Mesh
from jax.sharding import PartitionSpec as P

HEAD = 128
SEQ = ("seq_0", "seq_1", "seq_2")


EPS = 1e-06


def neutral_like(value, identity):
    return jax.tree.map(
        lambda part, zero: jnp.zeros_like(part) + jnp.asarray(zero, part.dtype), value, identity
    )


def entering(value, axes, combine, identity, reverse):
    before = start = neutral_like(value, identity)
    so_far = value
    for axis in reversed(axes):
        devices, index = (lax.axis_size(axis), lax.axis_index(axis))
        pieces = jax.tree.map(
            lambda part, kind: lax.all_gather(part.astype(kind), axis),
            so_far,
            (jnp.bfloat16, jnp.bfloat16),
        )
        inside, so_far = (start, start)
        for k in reversed(range(devices)) if reverse else range(devices):
            passed = k > index if reverse else k < index
            so_far = combine(
                so_far, jax.tree.map(lambda part, own: part[k].astype(own.dtype), pieces, value)
            )
            inside = jax.tree.map(lambda new, old: jnp.where(passed, new, old), so_far, inside)
        before = combine(inside, before)
    return before


def over_pieces(value, axis):
    parts = lax.all_gather(value, axis)
    return parts.sum(axis=0)


def from_behind(value, axis, steps):
    count = lax.axis_size(axis)
    pairs = [(source, (source + steps) % count) for source in range(count)]
    return lax.ppermute(value, axis, pairs)


def in_order(parts, dim):
    dims = list(parts.shape[1:])
    dims[dim] *= parts.shape[0]
    return jnp.moveaxis(parts, 0, dim).reshape(dims)


def from_everyone(value, axis):
    devices = lax.axis_size(axis)
    return lax.all_to_all(
        jnp.broadcast_to(value[None], (devices, *value.shape)), axis, 0, 0, tiled=True
    )


def collect(value, axis, dim):
    return in_order(from_everyone(value, axis), dim)


def linked(earlier, later_part):
    return (
        earlier[0] + later_part[0],
        jnp.exp(later_part[0])[:, None, None] * earlier[1] + later_part[1],
    )


def local(queries, keys, values, upstream, out_weight, gain, log_decay):
    tokens = queries.shape[1]
    local_width = queries.shape[2]
    heads_here = local_width // HEAD
    features = local_width * lax.axis_size("tp")
    query_rows = queries[0].reshape(tokens, heads_here, HEAD)
    key_rows = keys[0].reshape(tokens, heads_here, HEAD)
    value_rows = values[0].reshape(tokens, heads_here, HEAD)
    cumulative = jnp.cumsum(log_decay[0], axis=1)
    block_total = cumulative[:, -1]
    row_ids = lax.broadcasted_iota(jnp.int32, (tokens, tokens), 0)
    col_ids = lax.broadcasted_iota(jnp.int32, (tokens, tokens), 1)
    causal = (row_ids >= col_ids)[None]
    spread = cumulative[:, :, None] - cumulative[:, None, :]
    decay_mat = jnp.where(causal, jnp.exp(jnp.where(causal, spread, 0.0)), 0.0)
    scores = jnp.einsum("thd,shd->hts", query_rows, key_rows, preferred_element_type=jnp.float32)
    masked = (scores * decay_mat).astype(jnp.bfloat16)
    tail_decay = jnp.exp(block_total[:, None] - cumulative).T
    head_decay = jnp.exp(cumulative).T
    weighted_keys = (key_rows * tail_decay[:, :, None]).astype(jnp.bfloat16)
    local_state = jnp.einsum(
        "thd,the->hde", weighted_keys, value_rows, preferred_element_type=jnp.float32
    )
    zero_state = jnp.zeros((heads_here, HEAD, HEAD), jnp.float32)
    state_in = entering(
        (block_total, local_state), SEQ, linked, (jnp.zeros_like(block_total), zero_state), False
    )[1]
    state_bf = state_in.astype(jnp.bfloat16)
    attended = jnp.einsum("hts,shd->thd", masked, value_rows, preferred_element_type=jnp.float32)
    attended = attended + head_decay[:, :, None] * jnp.einsum(
        "thd,hde->the", query_rows, state_bf, preferred_element_type=jnp.float32
    )
    flat_out = attended.reshape(tokens, local_width)
    squares = jnp.sum(flat_out * flat_out, axis=1)
    square_total = over_pieces(squares, "tp")
    received = from_behind(upstream, "pp", -1)
    weight_rows = out_weight[0]
    grad_hidden = lax.dot_general(
        collect(received[0], "tp", 1),
        weight_rows,
        (((1,), (1,)), ((), ())),
        preferred_element_type=jnp.float32,
    )
    grad_norm = grad_hidden * gain[0][None, :]
    crossed = jnp.sum(grad_norm * flat_out, axis=1)
    cross_total = over_pieces(crossed, "tp")
    inverse = 1.0 / jnp.sqrt(square_total / features + EPS)
    factor = inverse * inverse * inverse * (cross_total / features)
    grad_attn = (inverse[:, None] * grad_norm - factor[:, None] * flat_out).astype(jnp.bfloat16)
    grad_attn = grad_attn.reshape(tokens, heads_here, HEAD)
    dscore = jnp.einsum("thd,shd->hts", grad_attn, value_rows, preferred_element_type=jnp.float32)
    dmask = (dscore * decay_mat).astype(jnp.bfloat16)
    weighted_queries = (query_rows * head_decay[:, :, None]).astype(jnp.bfloat16)
    passed = jnp.einsum(
        "thd,the->hde", weighted_queries, grad_attn, preferred_element_type=jnp.float32
    )
    later_state = entering(
        (block_total, passed), SEQ, linked, (jnp.zeros_like(block_total), zero_state), True
    )[1]
    later_bf = later_state.astype(jnp.bfloat16)
    grad_q = jnp.einsum("hts,shd->thd", dmask, key_rows, preferred_element_type=jnp.float32)
    grad_q = grad_q + head_decay[:, :, None] * jnp.einsum(
        "the,hde->thd", grad_attn, state_bf, preferred_element_type=jnp.float32
    )
    grad_k = jnp.einsum("hts,thd->shd", dmask, query_rows, preferred_element_type=jnp.float32)
    grad_k = grad_k + tail_decay[:, :, None] * jnp.einsum(
        "the,hde->thd", value_rows, later_bf, preferred_element_type=jnp.float32
    )
    grad_v = jnp.einsum("hts,thd->shd", masked, grad_attn, preferred_element_type=jnp.float32)
    grad_v = grad_v + tail_decay[:, :, None] * jnp.einsum(
        "thd,hde->the", key_rows, later_bf, preferred_element_type=jnp.float32
    )
    out_shape = (1, tokens, local_width)
    return (
        grad_q.astype(jnp.bfloat16).reshape(out_shape),
        grad_k.astype(jnp.bfloat16).reshape(out_shape),
        grad_v.astype(jnp.bfloat16).reshape(out_shape),
    )


def solution(mesh):
    torus = Mesh(
        mesh.devices.reshape(4, 4, 2, mesh.shape["tp"], mesh.shape["pp"]),
        ("seq_0", "seq_1", "seq_2", "tp", "pp"),
    )
    placed = (
        P("pp", SEQ, "tp"),
        P("pp", SEQ, "tp"),
        P("pp", SEQ, "tp"),
        P("pp", SEQ, "tp"),
        P("pp", "tp", None),
        P("pp", "tp"),
        P("pp", "tp", SEQ),
    )
    return jax.shard_map(
        local,
        mesh=torus,
        in_specs=placed,
        out_specs=(P("pp", SEQ, "tp"), P("pp", SEQ, "tp"), P("pp", SEQ, "tp")),
        check_vma=False,
    )
```

profile of v0, /device:TPU:1, one launch (start us, length us, event | category | flops | bytes accessed | tf_op | source)
XLA Modules:
  0.0 304.0 jit_solution(8770925223880888798)
XLA Ops:
  7.2 0.0 all-gather.25.cloned.1.call-start
  7.2 0.8 reshape.332
  8.0 1.2 reduce-window.6
  9.1 0.2 slice_reduce_fusion
  9.3 0.1 copy_bitcast_fusion
  9.4 0.2 slice_reduce_fusion.1
  9.6 0.1 exponential_bitcast_fusion.1
  9.7 2.9 copy.85
  12.6 3.0 copy.116
  15.6 1.3 copy-done.6
  16.9 2.2 fusion.19
  19.1 0.0 all-gather.25.cloned.1.call-update
  19.1 0.0 all-gather.17.cloned.1.call-start
  19.2 0.6 dynamic-slice
  20.4 0.2 fusion.85
  20.6 0.2 dynamic-update-slice
  20.8 4.3 %all-reduce = bf16[32]{0:T(256)(128)(2,1)S(1)} all-reduce(bf16[32]{0:T(256)(128)(2,1)S(1)} %dynamic-update-slice), channel_id=2, replica_groups=mesh['seq_0'=4,'seq_1'=4,'seq_2'=2,'tp'=2,'pp'=2] {'seq_2'}, use_global_device_ids=true, to_apply=%add | all-reduce | flops 32 | bytes 128
  25.2 0.1 convert_exponential_fusion.1
  25.2 20.8 %all-gather.25.cloned.1.call-done = bf16[32,128,128]{2,1,0:T(8,128)(2,1)} async-done(((bf16[16,128,128]{2,1,0:T(8,128)(2,1)}), bf16[32,128,128]{2,1,0:T(8,128)(2,1)}) %all-gather.25.cloned.1.call-update) | async-done | bytes 1048592 | tf_op jit(solution)/shard_map/all_gather | solution.py:26
  46.1 2.4 fusion.68
  48.5 0.0 all-gather.19.cloned.1.call-start
  48.6 7.7 %all-gather.5 = bf16[4,1,16]{2,1,0:T(2,128)(2,1)S(1)} all-gather(bf16[1,1,16]{2,1,0:T(2,128)(2,1)S(1)} %get-tuple-element.43), channel_id=1, replica_groups=mesh['seq_0'=4,'seq_1'=4,'seq_2'=2,'tp'=2,'pp'=2] {'seq_1'}, dimensions={0}, use_global_device_ids=true | all-gather | bytes 160 | tf_op jit(solution)/shard_map/all_gather | solution.py:26
  56.3 0.1 fusion.90
  56.3 24.1 %all-gather.17.cloned.1.call-done = bf16[4,16,128,128]{3,2,1,0:T(8,128)(2,1)} async-done(((bf16[1,16,128,128]{3,2,1,0:T(8,128)(2,1)}), bf16[4,16,128,128]{3,2,1,0:T(8,128)(2,1)}) %all-gather.17.cloned.1.call-update) | async-done | bytes 2097168 | tf_op jit(solution)/shard_map/all_gather | solution.py:26
  80.4 2.9 fusion.48
  83.3 2.8 collective-permute-start
  86.1 8.7 %all-gather.6 = bf16[4,1,16]{2,1,0:T(2,128)(2,1)S(1)} all-gather(bf16[1,1,16]{2,1,0:T(2,128)(2,1)S(1)} %get-tuple-element.26), channel_id=1, replica_groups=mesh['seq_0'=4,'seq_1'=4,'seq_2'=2,'tp'=2,'pp'=2] {'seq_0'}, dimensions={0}, use_global_device_ids=true | all-gather | bytes 160 | tf_op jit(solution)/shard_map/all_gather | solution.py:26
  94.8 0.1 fusion.88
  94.9 3.9 %copy.84 = bf16[1,512,2048]{1,2,0:T(8,128)(2,1)} copy(bf16[1,512,2048]{2,1,0:T(8,128)(2,1)} %param.7) | data formatting | bytes 4194304 | tf_op args[0]
  98.8 0.1 iota_compare_fusion
  98.9 6.7 %multiply_convert_fusion.1 = bf16[16,512,512]{2,1,0:T(8,128)(2,1)S(1)} fusion(bf16[512,16,128]{0,2,1:T(8,128)(2,1)} %bitcast.355, bf16[512,16,128]{0,2,1:T(8,128)(2,1)S(1)} %bitcast.348, f32[16,512]{1,0:T(8,128)S(1)} %copy_bitcast_fusion, pred[512,512]{1,0:T(8,128)(4,1)S(1)} %iota_compare_fusion), kind=kOutput, calls=%fused_computation.1 | convolution fusion | flops 1094713344 | bytes 12877824 | tf_op jit(solution)/shard_map/thd,shd->hts/dot_general | solution.py:91
  105.7 8.1 %fusion.13 = f32[16,512,128]{1,2,0:T(8,128)} fusion(bf16[16,512,512]{2,1,0:T(8,128)(2,1)S(1)} %multiply_convert_fusion.1, bf16[512,16,128]{2,1,0:T(8,128)(2,1)} %bitcast.352), kind=kOutput, calls=%fused_computation.25 | convolution fusion | flops 1073741824 | bytes 14680064 | tf_op jit(solution)/shard_map/hts,shd->thd/dot_general | solution.py:104
  113.8 6.6 %collective-permute-done = bf16[1,512,1536]{2,1,0:T(8,128)(2,1)} collective-permute-done((bf16[1,512,1536]{2,1,0:T(8,128)(2,1)}, bf16[1,512,1536]{2,1,0:T(8,128)(2,1)}, u32[]{:S(2)}, u32[]{:S(2)}) %collective-permute-start) | collective-permute-done | bytes 1572896 | tf_op jit(solution)/shard_map/ppermute | solution.py:49
  120.3 1.7 copy.94
  122.1 1.9 broadcast_in_dim.28
  124.0 6.9 %all-to-all-start = ((bf16[2,512,1536]{1,2,0:T(8,128)(2,1)}), bf16[2,512,1536]{1,2,0:T(8,128)(2,1)}, u32[]{:S(2)}, u32[]{:S(2)}) async-start(bf16[2,512,1536]{1,2,0:T(8,128)(2,1)} %broadcast_in_dim.28), calls=%async_computation | async-start | bytes 6291456 | tf_op jit(solution)/shard_map/all_to_all | solution.py:60
  130.9 4.6 %fusion.34 = bf16[16,128,128]{2,1,0:T(8,128)(2,1)S(1)} fusion(bf16[4,16,128,128]{3,2,1,0:T(8,128)(2,1)} %all-gather.19.cloned.1.call-done, f32[16]{0:T(128)S(1)} %get-tuple-element.41, f32[16]{0:T(128)S(1)} %get-tuple-element.42, f32[16]{0:T(128)S(1)} %get-tuple-element.28, f32[16]{0:T(128)S(1)} %get-tuple-element.29, f32[16]{0:T(128)S(1)} %get-tuple-element.30, ...), kind=kLoop, calls=%fused_computation.68 | loop fusion | flops 11010048 | bytes 5767946 | tf_op jit(solution)/shard_map/convert_element_type | solution.py:103
  135.5 5.0 %multiply_reduce_fusion.1 = (f32[512]{0:T(512)S(1)}, f32[512,16,128]{0,2,1:T(8,128)}) fusion(bf16[16,128,128]{2,1,0:T(8,128)(2,1)S(1)} %fusion.34, bf16[512,16,128]{0,2,1:T(8,128)(2,1)S(1)} %bitcast.357, f32[512,16]{0,1:T(8,128)S(1)} %get-tuple-element.19, f32[16,512,128]{1,2,0:T(8,128)} %fusion.13), kind=kOutput, calls=%fused_computation.19 | convolution fusion | flops 272629248 | bytes 11044864 | tf_op jit(solution)/shard_map/thd,hde->the/dot_general | solution.py:105
  140.5 5.4 %copy.95 = f32[512,2048]{1,0:T(8,128)} copy(f32[512,2048]{0,1:T(8,128)} %bitcast.359) | data formatting | bytes 8388608 | tf_op jit(solution)/shard_map/reshape | solution.py:108
  145.9 14.1 %multiply_reduce_fusion = (f32[512]{0:T(512)S(1)}, f32[512,2048]{1,0:T(8,128)}) fusion(f32[512,2048]{1,0:T(8,128)} %copy.95, f32[2048]{0:T(1024)S(1)} %bitcast.365, bf16[512,3072]{0,1:T(8,128)(2,1)} %bitcast.34, bf16[1,2048,3072]{2,1,0:T(8,128)(2,1)} %param.11), kind=kOutput, calls=%fused_computation.18 | convolution fusion | flops 6445596160 | bytes 24127488 | tf_op jit(solution)/shard_map/dot_general | solution.py:113
  160.1 1.8 all-gather.8
  161.9 1.8 all-gather.7
  163.8 5.5 %subtract_convert_fusion = bf16[512,2048]{1,0:T(8,128)(2,1)} fusion(f32[512,2048]{1,0:T(8,128)} %copy.95, f32[512,2048]{1,0:T(8,128)} %get-tuple-element.47, f32[512]{0:T(512)S(1)} %get-tuple-element.34, f32[2048]{0:T(1024)S(1)} %bitcast.366, f32[512]{0:T(512)S(1)} %get-tuple-element.33), kind=kLoop, calls=%fused_computation.17 | loop fusion | flops 5242880 | bytes 10498048 | tf_op jit(solution)/shard_map/convert_element_type | solution.py:124
  169.3 2.9 copy.114
  172.1 3.1 %fusion.22 = bf16[16,128,128]{2,1,0:T(8,128)(2,1)} fusion(bf16[512,16,128]{0,2,1:T(8,128)(2,1)S(1)} %bitcast.343, bf16[512,16,128]{0,2,1:T(8,128)(2,1)} %bitcast.356, f32[512,16]{0,1:T(8,128)S(1)} %get-tuple-element.19), kind=kOutput, calls=%fused_computation.56 | convolution fusion | flops 271843328 | bytes 4751360 | tf_op jit(solution)/shard_map/thd,the->hde/dot_general | solution.py:129
  175.2 0.0 all-gather.21.cloned.1.call-start
  175.3 23.3 %all-gather.27.cloned.1.call-done = bf16[32,128,128]{2,1,0:T(8,128)(2,1)} async-done(((bf16[16,128,128]{2,1,0:T(8,128)(2,1)}), bf16[32,128,128]{2,1,0:T(8,128)(2,1)}) %all-gather.27.cloned.1.call-update) | async-done | bytes 1048592 | tf_op jit(solution)/shard_map/all_gather | solution.py:26
  198.6 2.4 fusion.72
  201.1 0.0 all-gather.23.cloned.1.call-start
  201.1 31.9 %all-gather.21.cloned.1.call-done = bf16[4,16,128,128]{3,2,1,0:T(8,128)(2,1)} async-done(((bf16[1,16,128,128]{3,2,1,0:T(8,128)(2,1)}), bf16[4,16,128,128]{3,2,1,0:T(8,128)(2,1)}) %all-gather.21.cloned.1.call-update) | async-done | bytes 2097168 | tf_op jit(solution)/shard_map/all_gather | solution.py:26
  233.0 2.9 fusion.63
  235.9 8.1 %all-gather.9 = bf16[4,1,16]{2,1,0:T(2,128)(2,1)S(1)} all-gather(bf16[1,1,16]{2,1,0:T(2,128)(2,1)S(1)} %get-tuple-element.25), channel_id=1, replica_groups=mesh['seq_0'=4,'seq_1'=4,'seq_2'=2,'tp'=2,'pp'=2] {'seq_0'}, dimensions={0}, use_global_device_ids=true | all-gather | bytes 160 | tf_op jit(solution)/shard_map/all_gather | solution.py:26
  244.1 7.3 %multiply_convert_fusion = bf16[16,512,512]{2,1,0:T(8,128)(2,1)S(1)} fusion(bf16[512,16,128]{0,2,1:T(8,128)(2,1)S(1)} %bitcast.344, f32[16,512]{1,0:T(8,128)S(1)} %copy_bitcast_fusion, pred[512,512]{1,0:T(8,128)(4,1)S(1)} %iota_compare_fusion, bf16[512,16,128]{2,1,0:T(8,128)(2,1)} %bitcast.353), kind=kOutput, calls=%fused_computation | convolution fusion | flops 1094713344 | bytes 12877824 | tf_op jit(solution)/shard_map/thd,shd->hts/dot_general | solution.py:126
  251.4 4.8 %fusion.113 = f32[16,512,128]{1,2,0:T(8,128)} fusion(bf16[16,512,512]{2,1,0:T(8,128)(2,1)S(1)} %multiply_convert_fusion, bf16[512,16,128]{0,2,1:T(8,128)(2,1)S(1)} %bitcast.349), kind=kOutput, calls=%fused_computation.218 | convolution fusion | flops 1073741824 | bytes 14680064 | tf_op jit(solution)/shard_map/hts,shd->thd/dot_general | solution.py:136
  256.2 4.3 %fusion.7 = bf16[512,16,128]{0,2,1:T(8,128)(2,1)} fusion(f32[16,512,128]{1,2,0:T(8,128)} %fusion.113, bf16[16,128,128]{2,1,0:T(8,128)(2,1)S(1)} %fusion.34, bf16[512,16,128]{0,2,1:T(8,128)(2,1)S(1)} %bitcast.345, f32[512,16]{0,1:T(8,128)S(1)} %get-tuple-element.19), kind=kOutput, calls=%fused_computation.13 | convolution fusion | flops 271581184 | bytes 8945664 | tf_op jit(solution)/shard_map/the,hde->thd/dot_general | solution.py:137
  260.4 3.9 %copy.105 = bf16[1,512,2048]{2,1,0:T(8,128)(2,1)} copy(bf16[1,512,2048]{1,2,0:T(8,128)(2,1)} %bitcast.360) | data formatting | bytes 4194304
  264.3 6.7 %fusion.114 = f32[16,128,512]{2,1,0:T(8,128)} fusion(bf16[512,16,128]{0,2,1:T(8,128)(2,1)S(1)} %bitcast.346, bf16[16,512,512]{2,1,0:T(8,128)(2,1)} %copy-done), kind=kOutput, calls=%fused_computation.219 | convolution fusion | flops 1073741824 | bytes 14680064 | tf_op jit(solution)/shard_map/hts,thd->shd/dot_general | solution.py:144
  271.0 4.4 %fusion.30 = bf16[16,128,128]{2,1,0:T(8,128)(2,1)S(1)} fusion(bf16[4,16,128,128]{3,2,1,0:T(8,128)(2,1)} %all-gather.23.cloned.1.call-done, f32[16]{0:T(128)S(1)} %get-tuple-element.39, f32[16]{0:T(128)S(1)} %get-tuple-element.40, f32[16]{0:T(128)S(1)} %get-tuple-element.27, f32[16]{0:T(128)S(1)} %get-tuple-element.31, f32[16]{0:T(128)S(1)} %exp.195, ...), kind=kLoop, calls=%fused_computation.64 | loop fusion | flops 11010048 | bytes 5767946 | tf_op jit(solution)/shard_map/convert_element_type | solution.py:135
  275.5 3.1 %fusion.15 = f32[16,128,512]{2,1,0:T(8,128)} fusion(bf16[16,128,128]{2,1,0:T(8,128)(2,1)S(1)} %fusion.30, bf16[512,16,128]{2,1,0:T(8,128)(2,1)S(1)} %bitcast.354), kind=kOutput, calls=%fused_computation.27 | convolution fusion | flops 268435456 | bytes 6815744 | tf_op jit(solution)/shard_map/the,hde->thd/dot_general | solution.py:141
  278.6 1.2 copy-done.5
  279.9 2.1 fusion.3
  282.0 4.1 %copy.107 = bf16[1,512,2048]{2,1,0:T(8,128)(2,1)} copy(bf16[1,512,2048]{1,2,0:T(8,128)(2,1)} %bitcast.361) | data formatting | bytes 4194304
  286.0 7.2 %fusion.5 = bf16[512,16,128]{0,2,1:T(8,128)(2,1)} fusion(f32[16,128,512]{2,1,0:T(8,128)} %fusion.15, bf16[512,16,128]{0,2,1:T(8,128)(2,1)S(1)} %bitcast.358, bf16[16,512,512]{2,1,0:T(8,128)(2,1)} %copy-done.1, f32[512,16]{0,1:T(8,128)S(1)} %get-tuple-element.20), kind=kOutput, calls=%fused_computation.10 | convolution fusion | flops 1076887552 | bytes 16809984 | tf_op jit(solution)/shard_map/hts,thd->shd/dot_general | solution.py:140
  293.2 3.9 %copy.106 = bf16[1,512,2048]{2,1,0:T(8,128)(2,1)} copy(bf16[1,512,2048]{1,2,0:T(8,128)(2,1)} %bitcast.362) | data formatting | bytes 4194304
  (45 shorter events, 0.3 us)
Async XLA Ops:
  7.2 38.9 %all-gather.25.cloned.1.call-start = ((), (), s32[]{:S(2)}) async-start(), calls=%async_computation.5 | async-start | bytes 1572864 | tf_op jit(solution)/shard_map/all_gather | solution.py:26
  12.6 86.3 %copy-start.3 = (bf16[1,512,2048]{1,2,0:T(8,128)(2,1)}, bf16[1,512,2048]{1,2,0:T(8,128)(2,1)S(1)}, u32[]{:S(2)}) copy-start(bf16[1,512,2048]{1,2,0:T(8,128)(2,1)S(1)} %copy.85) | copy-start | bytes 6291460
  15.6 1.3 copy-start.6
  15.6 3.6 %copy-start.12 = (u32[128]{0:T(128)S(1)}, u32[128]{0:T(128)}, u32[]{:S(2)}) copy-start(u32[128]{0:T(128)} %constant.45) | copy-start | bytes 1540
  19.1 61.3 %all-gather.17.cloned.1.call-start = ((), (), s32[]{:S(2)}) async-start(), calls=%async_computation.1 | async-start | bytes 2621440 | tf_op jit(solution)/shard_map/all_gather | solution.py:26
  48.5 82.4 %all-gather.19.cloned.1.call-start = ((), (), s32[]{:S(2)}) async-start(), calls=%async_computation.2 | async-start | bytes 2621440 | tf_op jit(solution)/shard_map/all_gather | solution.py:26
  83.3 37.0 %collective-permute-start = (bf16[1,512,1536]{2,1,0:T(8,128)(2,1)}, bf16[1,512,1536]{2,1,0:T(8,128)(2,1)}, u32[]{:S(2)}, u32[]{:S(2)}) collective-permute-start(bf16[1,512,1536]{2,1,0:T(8,128)(2,1)} %param.10), channel_id=1, source_target_pairs={{0,1},{1,0},{2,3},{3,2},{4,5},{5,4},{6,7},{7,6},{8,9},{9,8},{10,11... | collective-permute-start | bytes 4718600 | tf_op jit(solution)/shard_map/ppermute | solution.py:49
  105.7 8.1 %copy-start = (bf16[16,512,512]{2,1,0:T(8,128)(2,1)}, bf16[16,512,512]{2,1,0:T(8,128)(2,1)S(1)}, u32[]{:S(2)}) copy-start(bf16[16,512,512]{2,1,0:T(8,128)(2,1)S(1)} %multiply_convert_fusion.1) | copy-start | bytes 25165828
  124.0 21.9 %all-to-all-start = ((bf16[2,512,1536]{1,2,0:T(8,128)(2,1)}), bf16[2,512,1536]{1,2,0:T(8,128)(2,1)}, u32[]{:S(2)}, u32[]{:S(2)}) async-start(bf16[2,512,1536]{1,2,0:T(8,128)(2,1)} %broadcast_in_dim.28), calls=%async_computation | async-start | bytes 6291456 | tf_op jit(solution)/shard_map/all_to_all | solution.py:60
  130.9 4.6 %copy-start.8 = (bf16[1,512,2048]{1,2,0:T(8,128)(2,1)S(1)}, bf16[1,512,2048]{1,2,0:T(8,128)(2,1)}, u32[]{:S(2)}) copy-start(bf16[1,512,2048]{1,2,0:T(8,128)(2,1)} %copy.84) | copy-start | bytes 6291460
  130.9 67.8 %all-gather.27.cloned.1.call-start = ((), (), s32[]{:S(2)}) async-start(), calls=%async_computation.6 | async-start | bytes 1572864 | tf_op jit(solution)/shard_map/all_gather | solution.py:26
  140.5 5.4 %copy-start.11 = (f32[1,2048]{1,0:T(1,128)S(1)}, f32[1,2048]{1,0:T(1,128)}, u32[]{:S(2)}) copy-start(f32[1,2048]{1,0:T(1,128)} %param.12) | copy-start | bytes 24580
  175.2 57.8 %all-gather.21.cloned.1.call-start = ((), (), s32[]{:S(2)}) async-start(), calls=%async_computation.3 | async-start | bytes 2621440 | tf_op jit(solution)/shard_map/all_gather | solution.py:26
  201.1 69.9 %all-gather.23.cloned.1.call-start = ((), (), s32[]{:S(2)}) async-start(), calls=%async_computation.4 | async-start | bytes 2621440 | tf_op jit(solution)/shard_map/all_gather | solution.py:26
  244.1 7.3 %copy-start.4 = (bf16[1,512,2048]{1,2,0:T(8,128)(2,1)S(1)}, bf16[1,512,2048]{1,2,0:T(8,128)(2,1)}, u32[]{:S(2)}) copy-start(bf16[1,512,2048]{1,2,0:T(8,128)(2,1)} %copy-done.3) | copy-start | bytes 6291460
  251.4 4.8 %copy-start.1 = (bf16[16,512,512]{2,1,0:T(8,128)(2,1)}, bf16[16,512,512]{2,1,0:T(8,128)(2,1)S(1)}, u32[]{:S(2)}) copy-start(bf16[16,512,512]{2,1,0:T(8,128)(2,1)S(1)} %multiply_convert_fusion) | copy-start | bytes 25165828
  264.3 6.7 %copy-start.10 = (bf16[32,128,128]{2,1,0:T(8,128)(2,1)S(1)}, bf16[32,128,128]{2,1,0:T(8,128)(2,1)}, u32[]{:S(2)}) copy-start(bf16[32,128,128]{2,1,0:T(8,128)(2,1)} %all-gather.27.cloned.1.call-done) | copy-start | bytes 3145732
  271.0 4.5 %copy-start.7 = (bf16[64,8,16,128]{3,2,1,0:T(8,128)(2,1)S(1)}, bf16[64,8,16,128]{3,2,1,0:T(8,128)(2,1)}, u32[]{:S(2)}) copy-start(bf16[64,8,16,128]{3,2,1,0:T(8,128)(2,1)} %copy-done.6) | copy-start | bytes 6291460
  275.5 3.1 %copy-start.2 = (f32[16,128,512]{2,1,0:T(8,128)S(1)}, f32[16,128,512]{2,1,0:T(8,128)}, u32[]{:S(2)}) copy-start(f32[16,128,512]{2,1,0:T(8,128)} %fusion.114) | copy-start | bytes 12582916
  275.5 4.4 %copy-start.5 = (bf16[1,512,2048]{1,2,0:T(8,128)(2,1)S(1)}, bf16[1,512,2048]{1,2,0:T(8,128)(2,1)}, u32[]{:S(2)}) copy-start(bf16[1,512,2048]{1,2,0:T(8,128)(2,1)} %copy-done.3) | copy-start | bytes 6291460
  282.0 4.1 %copy-start.9 = (bf16[1,512,2048]{1,2,0:T(8,128)(2,1)S(1)}, bf16[1,512,2048]{1,2,0:T(8,128)(2,1)}, u32[]{:S(2)}) copy-start(bf16[1,512,2048]{1,2,0:T(8,128)(2,1)} %copy.84) | copy-start | bytes 6291460
Sparse Core Ops, SparseCore 0:
  19.2 26.8 all-gather.24
  48.6 31.7 all-gather.16
  83.5 30.9 all-gather.18
  175.4 23.2 all-gather.26
  201.2 31.7 all-gather.20
  236.0 30.9 all-gather.22
where the time goes:
time: 307 us; the launch traced here: 304 us
  waiting for transfers between devices  107 us (35%)
  matrix products  74.7 us (24%)
  local copies, waits for them, and re-layouts  38.3 us (12%)
  blocking collectives  32.5 us (11%)
  other arithmetic  26.9 us (9%)
  between operations  15 us (5%)
  starting transfers between devices  9.88 us (3%)
    all_gather x6, waiting for transfers between devices, entering(): lax.all_gather(part.astype(kind), axis)  100 us
    unnamed x35, local copies, waits for them, and re-layouts  25.1 us
    all_gather x3, blocking collectives, entering(): lax.all_gather(part.astype(kind), axis)  24.5 us
    dot_general x1, matrix products, local(): lax.dot_general(collect(received[0], 'tp', 1), weight_rows, (((1,), (1,))...  14.1 us
    convert_element_type x4, other arithmetic, entering(): part.astype(kind)  10.6 us
    dot_general x1, matrix products, local(): jnp.einsum('hts,shd->thd', masked, value_rows, preferred_element_type=jnp...  8.06 us
    dot_general x1, matrix products, local(): jnp.einsum('thd,shd->hts', grad_attn, value_rows, preferred_element_type=...  7.3 us
    dot_general x1, matrix products, local(): jnp.einsum('hts,thd->shd', dmask, query_rows, preferred_element_type=jnp....  7.2 us
  transfers between devices with their start and end apart: 8, of which 5 were waited for; matrix products, arithmetic and copies ran while one was open for 22% of the time, Pallas kernels for 0%

commit v1 on v0

v1 whole, which is shorter than its diff:
```python
import jax
import jax.numpy as jnp
from jax import lax
from jax.experimental import pallas as pl
from jax.experimental.pallas import tpu as pltpu
from jax.sharding import Mesh
from jax.sharding import PartitionSpec as P

HEAD = 128
SEQ = ("seq_0", "seq_1", "seq_2")
MESH = pl.DeviceIdType.MESH
EPS = 1e-06
BF = jnp.bfloat16
F32 = jnp.float32

TOK = 512
HALF = 256
WIDTH = 2048
HEADS = 16
MODEL = 3072
CHUNKS = 6
CW = 256
BLOCKS = 32
ROWS = 64
FEATURES = 4096


def nn(a, b):
    return lax.dot_general(a, b, (((1,), (0,)), ((), ())), preferred_element_type=F32)


def nt(a, b):
    return lax.dot_general(a, b, (((1,), (1,)), ((), ())), preferred_element_type=F32)


def lanes(h):
    return pl.ds(pl.multiple_of(h * HEAD, HEAD), HEAD)


def kernel(
    q_hbm, k_hbm, v_hbm, up_hbm, w_hbm, gain_hbm, ld_hbm,
    dq_hbm, dk_hbm, dv_hbm,
    q, k, v, w, up, att, gh, ga, wqt, ccol, crow, mta, mtb,
    own_f, got_f, scan_f, state, own_b, got_b, scan_b, later,
    totals, tot_in, sq_own, sq_in, cr_own, cr_in, inv, fac, gain, ld,
    dqs, dks, dvs,
    load_sem, tot_sem, a2a_sem, perm_send, perm_recv, fwd_send, fwd_recv, tp_sem, out_sem,
):
    z, y, x = (lax.axis_index(a) for a in SEQ)
    me = z * 8 + y * 2 + x
    tp = lax.axis_index("tp")
    sibling = {"tp": 1 - tp}
    across = {"pp": 1 - lax.axis_index("pp")}

    def peer(i):
        p = lax.rem(me + i, BLOCKS)
        return p, {"seq_0": p // 8, "seq_1": lax.rem(p // 2, 4), "seq_2": lax.rem(p, 2)}

    loads = []

    def load(src, dst):
        copy = pltpu.make_async_copy(src, dst, load_sem.at[len(loads)])
        copy.start()
        loads.append(copy)
        return copy

    ld_load = load(ld_hbm.at[0], ld)
    k_load = load(k_hbm.at[0], k)
    v_load = load(v_hbm.at[0], v)
    q_load = load(q_hbm.at[0], q)
    gain_load = load(gain_hbm, gain)
    w_loads = []
    for j in range(CHUNKS):
        for part, side in enumerate((tp, 1 - tp)):
            at = pl.multiple_of(side * (MODEL // 2) + j * CW, CW)
            w_loads.append(
                load(w_hbm.at[0, :, pl.ds(at, CW)], w.at[:, pl.ds((2 * j + part) * CW, CW)])
            )

    barrier = pltpu.get_barrier_semaphore()

    @pl.loop(1, BLOCKS)
    def _(i):
        _, device = peer(i)
        pl.semaphore_signal(barrier, inc=1, device_id=device, device_id_type=MESH)

    pl.semaphore_signal(barrier, inc=1, device_id=sibling, device_id_type=MESH)
    pl.semaphore_signal(barrier, inc=1, device_id=across, device_id_type=MESH)
    pl.semaphore_wait(barrier, BLOCKS + 1)

    def permute(j):
        return pltpu.make_async_remote_copy(
            src_ref=up_hbm.at[0, :, pl.ds(j * CW, CW)],
            dst_ref=up.at[:, pl.ds(2 * j * CW, CW)],
            send_sem=perm_send.at[j],
            recv_sem=perm_recv.at[j],
            device_id=across,
            device_id_type=MESH,
        )

    def forward(j):
        return pltpu.make_async_remote_copy(
            src_ref=up.at[:, pl.ds(2 * j * CW, CW)],
            dst_ref=up.at[:, pl.ds((2 * j + 1) * CW, CW)],
            send_sem=fwd_send.at[j],
            recv_sem=fwd_recv.at[j],
            device_id=sibling,
            device_id_type=MESH,
        )

    def exchange(src, dst, send_sem, recv_sem):
        @pl.loop(1, BLOCKS)
        def _(i):
            p, device = peer(i)
            pltpu.make_async_remote_copy(
                src_ref=src.at[p],
                dst_ref=dst.at[me],
                send_sem=send_sem,
                recv_sem=recv_sem,
                device_id=device,
                device_id_type=MESH,
            ).start()

        dst[me] = src[me]

    def arrived(ref, sem):
        whole = ref.at[pl.ds(0, BLOCKS - 1)]
        pltpu.make_async_copy(whole, whole, sem).wait()

    for j in (0, 1):
        permute(j).start()

    ld_load.wait()
    cum = ld[...]
    place = lax.broadcasted_iota(jnp.int32, (HEADS, TOK), 1)
    step = 1
    while step < TOK:
        moved = pltpu.roll(cum, step, 1)
        cum = cum + jnp.where(place >= step, moved, 0.0)
        step *= 2
    crow[...] = cum
    total = jnp.broadcast_to(cum[:, TOK - 1 : TOK], (HEADS, HEAD))
    for h in range(HEADS):
        totals[2 * h : 2 * h + 1, 0] = total[h : h + 1]
        totals[2 * h + 1 : 2 * h + 2, 0] = total[h : h + 1]
    exchange(totals, tot_in, tot_sem.at[0], tot_sem.at[1])
    turned = cum.T
    for h in range(HEADS):
        ccol[h] = jnp.broadcast_to(turned[:, h : h + 1], (TOK, HEAD))

    k_load.wait()
    v_load.wait()

    @pl.loop(0, HEADS)
    def _(h):
        tail = jnp.exp(totals[2 * h] - ccol[h])
        weighted = (k[:, lanes(h)].astype(F32) * tail).astype(BF)
        local_state = nn(weighted.T, v[:, lanes(h)]).astype(BF)
        own_f[2 * h] = local_state[:ROWS]
        own_f[2 * h + 1] = local_state[ROWS:]

    exchange(own_f, got_f, a2a_sem.at[0], a2a_sem.at[1])
    for j in (2, 3):
        permute(j).start()
    q_load.wait()

    lower = lax.broadcasted_iota(jnp.int32, (HALF, HALF), 0) >= lax.broadcasted_iota(
        jnp.int32, (HALF, HALF), 1
    )
    upper = lax.broadcasted_iota(jnp.int32, (HALF, HALF), 0) <= lax.broadcasted_iota(
        jnp.int32, (HALF, HALF), 1
    )
    low = -1e30

    def decay_parts(h):
        col = ccol[h]
        col2 = jnp.concatenate([col, col], axis=1)
        row = crow[pl.ds(h, 1), :]
        c0, c1 = col2[:HALF], col2[HALF:]
        r0, r1 = row[:, :HALF], row[:, HALF:]
        d00 = jnp.exp(jnp.where(lower, c0 - r0, low))
        d10 = jnp.exp(c1 - r0)
        d11 = jnp.exp(jnp.where(lower, c1 - r1, low))
        return d00, d10, d11

    def turned_parts(h):
        col = ccol[h]
        col2 = jnp.concatenate([col, col], axis=1)
        row = crow[pl.ds(h, 1), :]
        c0, c1 = col2[:HALF], col2[HALF:]
        r0, r1 = row[:, :HALF], row[:, HALF:]
        t00 = jnp.exp(jnp.where(upper, r0 - c0, low))
        t01 = jnp.exp(r1 - c0)
        t11 = jnp.exp(jnp.where(upper, r1 - c1, low))
        return t00, t01, t11

    @pl.loop(0, HEADS)
    def _(h):
        qh, kh, vh = q[:, lanes(h)], k[:, lanes(h)], v[:, lanes(h)]
        q0, q1, k0, k1 = qh[:HALF], qh[HALF:], kh[:HALF], kh[HALF:]
        d00, d10, d11 = decay_parts(h)
        m00 = (nt(q0, k0) * d00).astype(BF)
        m10 = (nt(q1, k0) * d10).astype(BF)
        m11 = (nt(q1, k1) * d11).astype(BF)
        att[:HALF, lanes(h)] = nn(m00, vh[:HALF])
        att[HALF:, lanes(h)] = nn(jnp.concatenate([m10, m11], axis=1), vh)
        t00, t01, t11 = turned_parts(h)
        mta[h, :, :HALF] = (nt(k0, q0) * t00).astype(BF)
        mta[h, :, HALF:] = (nt(k0, q1) * t01).astype(BF)
        mtb[h] = (nt(k1, q1) * t11).astype(BF)
        wq = (qh.astype(F32) * jnp.exp(ccol[h])).astype(BF)
        wqt[h] = wq.T

    arrived(tot_in, tot_sem.at[1])
    arrived(got_f, a2a_sem.at[1])
    running = jnp.zeros((ROWS, HEAD), F32)
    for b in range(BLOCKS):
        scan_f[b] = running.astype(BF)
        running = jnp.exp(tot_in[b]) * running + got_f[b].astype(F32)
    exchange(scan_f, state, a2a_sem.at[2], a2a_sem.at[3])
    for j in (4, 5):
        permute(j).start()

    gain_load.wait()
    for copy in w_loads:
        copy.wait()

    def hidden(j, first):
        @pl.loop(0, 4)
        def _(n):
            at = pl.ds(pl.multiple_of(n * 512, 512), 512)
            part = nt(up[:, 2 * j * CW : (2 * j + 2) * CW], w[at, 2 * j * CW : (2 * j + 2) * CW])
            if first:
                gh[:, at] = part
            else:
                gh[:, at] += part

    for j in (0, 1, 2):
        permute(j).wait_recv()
        forward(j).start()
    for j in (0, 1):
        forward(j).wait_recv()
        hidden(j, j == 0)

    arrived(state, a2a_sem.at[3])
    sq_own[...] = jnp.zeros_like(sq_own)

    @pl.loop(0, HEADS)
    def _(h):
        st = jnp.concatenate([state[2 * h], state[2 * h + 1]], axis=0)
        new = att[:, lanes(h)] + jnp.exp(ccol[h]) * nn(q[:, lanes(h)], st)
        att[:, lanes(h)] = new
        sq_own[...] += new * new

    def to_sibling(src, dst, i):
        return pltpu.make_async_remote_copy(
            src_ref=src,
            dst_ref=dst,
            send_sem=tp_sem.at[2 * i],
            recv_sem=tp_sem.at[2 * i + 1],
            device_id=sibling,
            device_id_type=MESH,
        )

    squares = to_sibling(sq_own, sq_in, 0)
    squares.start()
    for j in range(2, CHUNKS):
        if j > 2:
            permute(j).wait_recv()
            forward(j).start()
        forward(j).wait_recv()
        hidden(j, False)
        if j == 2:
            squares.wait_recv()
            square_total = jnp.sum(sq_own[...] + sq_in[...], axis=1, keepdims=True)
            inv[...] = jnp.broadcast_to(
                1.0 / jnp.sqrt(square_total / FEATURES + EPS), (TOK, HEAD)
            )

    cr_own[...] = jnp.zeros_like(cr_own)

    @pl.loop(0, HEADS)
    def _(h):
        norm = gh[:, lanes(h)] * gain[:, lanes(h)]
        gh[:, lanes(h)] = norm
        cr_own[...] += norm * att[:, lanes(h)]

    crossed = to_sibling(cr_own, cr_in, 1)
    crossed.start()
    crossed.wait_recv()
    cross_total = jnp.sum(cr_own[...] + cr_in[...], axis=1, keepdims=True)
    inverse = inv[...]
    fac[...] = inverse * inverse * inverse * jnp.broadcast_to(cross_total / FEATURES, (TOK, HEAD))

    @pl.loop(0, HEADS)
    def _(h):
        grad = (inv[...] * gh[:, lanes(h)] - fac[...] * att[:, lanes(h)]).astype(BF)
        ga[:, lanes(h)] = grad
        passed = nn(wqt[h], grad).astype(BF)
        own_b[2 * h] = passed[:ROWS]
        own_b[2 * h + 1] = passed[ROWS:]

    exchange(own_b, got_b, a2a_sem.at[4], a2a_sem.at[5])

    def put(src, dst, h, i):
        pltpu.make_async_copy(src.at[:, lanes(h)], dst.at[0, :, lanes(h)], out_sem.at[i]).start()

    def gradients(h):
        qh, kh, vh, gah = q[:, lanes(h)], k[:, lanes(h)], v[:, lanes(h)], ga[:, lanes(h)]
        v0, v1, g0, g1 = vh[:HALF], vh[HALF:], gah[:HALF], gah[HALF:]
        d00, d10, d11 = decay_parts(h)
        m00 = (nt(g0, v0) * d00).astype(BF)
        m10 = (nt(g1, v0) * d10).astype(BF)
        m11 = (nt(g1, v1) * d11).astype(BF)
        st = jnp.concatenate([state[2 * h], state[2 * h + 1]], axis=0)
        head = jnp.exp(ccol[h])
        dq0 = nn(m00, kh[:HALF])
        dq1 = nn(jnp.concatenate([m10, m11], axis=1), kh)
        inter = head * nt(gah, st)
        dqs[:HALF, lanes(h)] = (dq0 + inter[:HALF]).astype(BF)
        dqs[HALF:, lanes(h)] = (dq1 + inter[HALF:]).astype(BF)
        put(dqs, dq_hbm, h, 0)
        t00, t01, t11 = turned_parts(h)
        n0 = jnp.concatenate(
            [(nt(v0, g0) * t00).astype(BF), (nt(v0, g1) * t01).astype(BF)], axis=1
        )
        n1 = (nt(v1, g1) * t11).astype(BF)
        att[:HALF, lanes(h)] = nn(n0, qh)
        att[HALF:, lanes(h)] = nn(n1, qh[HALF:])
        gh[:HALF, lanes(h)] = nn(mta[h], gah)
        gh[HALF:, lanes(h)] = nn(mtb[h], g1)

    pl.loop(0, HEADS // 2)(gradients)

    arrived(got_b, a2a_sem.at[5])
    running = jnp.zeros((ROWS, HEAD), F32)
    for b in reversed(range(BLOCKS)):
        scan_b[b] = running.astype(BF)
        running = jnp.exp(tot_in[b]) * running + got_b[b].astype(F32)
    exchange(scan_b, later, a2a_sem.at[6], a2a_sem.at[7])

    pl.loop(HEADS // 2, HEADS)(gradients)

    arrived(later, a2a_sem.at[7])

    @pl.loop(0, HEADS)
    def _(h):
        lt = jnp.concatenate([later[2 * h], later[2 * h + 1]], axis=0)
        tail = jnp.exp(totals[2 * h] - ccol[h])
        dks[:, lanes(h)] = (att[:, lanes(h)] + tail * nt(v[:, lanes(h)], lt)).astype(BF)
        put(dks, dk_hbm, h, 1)
        dvs[:, lanes(h)] = (gh[:, lanes(h)] + tail * nn(k[:, lanes(h)], lt)).astype(BF)
        put(dvs, dv_hbm, h, 2)

    for i, (src, dst) in enumerate(((dqs, dq_hbm), (dks, dk_hbm), (dvs, dv_hbm))):
        pltpu.make_async_copy(src, dst.at[0], out_sem.at[i]).wait()
    arrived(totals, tot_sem.at[0])
    for i, ref in enumerate((own_f, scan_f, own_b, scan_b)):
        arrived(ref, a2a_sem.at[2 * i])
    for j in range(CHUNKS):
        permute(j).wait_send()
        forward(j).wait_send()
    squares.wait_send()
    crossed.wait_send()


def local(queries, keys, values, upstream, out_weight, gain, log_decay):
    piece = pltpu.VMEM((BLOCKS, ROWS, HEAD), BF)
    column = pltpu.VMEM((TOK, HEAD), F32)
    rows_bf = pltpu.VMEM((TOK, WIDTH), BF)
    rows_f32 = pltpu.VMEM((TOK, WIDTH), F32)
    dma = pltpu.SemaphoreType.DMA
    hbm = pl.BlockSpec(memory_space=pl.ANY)
    out = jax.ShapeDtypeStruct((1, TOK, WIDTH), BF)
    return pl.pallas_call(
        kernel,
        out_shape=(out, out, out),
        in_specs=[hbm] * 7,
        out_specs=[hbm] * 3,
        scratch_shapes=[
            rows_bf, rows_bf, rows_bf,
            pltpu.VMEM((WIDTH, MODEL), BF),
            pltpu.VMEM((TOK, MODEL), BF),
            rows_f32, rows_f32, rows_bf,
            pltpu.VMEM((HEADS, HEAD, TOK), BF),
            pltpu.VMEM((HEADS, TOK, HEAD), F32),
            pltpu.VMEM((HEADS, TOK), F32),
            pltpu.VMEM((HEADS, HALF, TOK), BF),
            pltpu.VMEM((HEADS, HALF, HALF), BF),
            piece, piece, piece, piece, piece, piece, piece, piece,
            pltpu.VMEM((BLOCKS, 1, HEAD), F32),
            pltpu.VMEM((BLOCKS, 1, HEAD), F32),
            column, column, column, column, column, column,
            pltpu.VMEM((1, WIDTH), F32),
            pltpu.VMEM((HEADS, TOK), F32),
            rows_bf, rows_bf, rows_bf,
            dma((5 + 2 * CHUNKS,)),
            dma((2,)),
            dma((8,)),
            dma((CHUNKS,)), dma((CHUNKS,)), dma((CHUNKS,)), dma((CHUNKS,)),
            dma((4,)),
            dma((3,)),
        ],
        compiler_params=pltpu.CompilerParams(
            collective_id=0, has_side_effects=True, vmem_limit_bytes=67043328
        ),
        name="decayed_backward",
    )(queries, keys, values, upstream, out_weight, gain, log_decay)


def solution(mesh):
    torus = Mesh(
        mesh.devices.reshape(4, 4, 2, mesh.shape["tp"], mesh.shape["pp"]),
        ("seq_0", "seq_1", "seq_2", "tp", "pp"),
    )
    rows = P("pp", SEQ, "tp")
    placed = (rows, rows, rows, rows, P("pp", "tp", None), P("pp", "tp"), P("pp", "tp", SEQ))
    return jax.shard_map(
        local, mesh=torus, in_specs=placed, out_specs=(rows, rows, rows), check_vma=False
    )
```

time: 307 us -> 97.5 us (0.32)
  waiting for transfers between devices: 107 us -> 0 us
  Pallas kernels: 0 us -> 88.3 us
  matrix products: 74.7 us -> 0 us
  blocking collectives: 32.5 us -> 0 us
  local copies, waits for them, and re-layouts: 38.3 us -> 6.98 us
  other arithmetic: 26.9 us -> 0 us
  between operations: 15 us -> 0.65 us
  starting transfers between devices: 9.88 us -> 0 us
    all_gather x6 -> x0, waiting for transfers between devices: 100 us -> none  [entering(): lax.all_gather(part.astype(kind), axis)]
    pallas_call x0 -> x1, Pallas kernels: none -> 88.3 us  [local(): pl.pallas_call(kernel, out_shape=(out, out, out), in_specs=[hbm] * 7, out...]
    dot_general x13 -> x0, matrix products: 74.7 us -> none  [the longest x1 14.1 us: local(): lax.dot_general(collect(received[0], 'tp', 1), weight_rows, (((1,), (1,))...]
    all_gather x5 -> x0, blocking collectives: 28.2 us -> none  [the longest x3 24.5 us: entering(): lax.all_gather(part.astype(kind), axis)]
    convert_element_type x7 -> x0, other arithmetic: 25.1 us -> none  [the longest x4 10.6 us: entering(): part.astype(kind)]
    unnamed x35 -> x7, local copies, waits for them, and re-layouts: 25.1 us -> 6.98 us
    reshape x4 -> x0, local copies, waits for them, and re-layouts: 9.02 us -> none  [the longest x1 5.38 us: local(): flat_out = attended.reshape(tokens, local_width)]
    all_to_all x1 -> x0, starting transfers between devices: 6.9 us -> none  [from_everyone(): lax.all_to_all(jnp.broadcast_to(value[None], (devices, *value.shape)), ax...]
  transfers between devices with their start and end apart: 8 -> 0, of which waited for: 5 -> 0; matrix products, arithmetic and copies ran while one was open for 22% -> 0% of each run, Pallas kernels for 0% -> 0%
where the time goes in v1:
time: 97.5 us; the launch traced here: 95.9 us
  Pallas kernels  88.3 us (91%)
  local copies, waits for them, and re-layouts  6.98 us (7%)
    pallas_call x1, Pallas kernels, local(): pl.pallas_call(kernel, out_shape=(out, out, out), in_specs=[hbm] * 7, out...  88.3 us
    unnamed x7, local copies, waits for them, and re-layouts  6.98 us

profile of v1, /device:TPU:1, one launch (start us, length us, event | category | flops | bytes accessed | tf_op | source)
XLA Modules:
  0.0 95.9 jit_solution(14445618684992905749)
XLA Ops:
  0.6 88.3 %decayed_backward.1 = (bf16[1,512,2048]{2,1,0:T(8,128)(2,1)}, bf16[1,512,2048]{2,1,0:T(8,128)(2,1)}, bf16[1,512,2048]{2,1,0:T(8,128)(2,1)}) custom-call(bf16[1,512,2048]{2,1,0:T(8,128)(2,1)} %q_hbm.1, bf16[1,512,2048]{2,1,0:T(8,128)(2,1)} %k_hbm.1, bf16[1,512,2048]{2,1,0:T(8,128)(2,1)} %v_hbm.1, bf16[1,512,1536]{2,1,0:T(8,128)(2,1)} %up_hbm.1, ...), custom_call_target="tpu_custom_call" | custom-call | tf_op jit(solution)/shard_map/decayed_backward/pallas_call | solution.py:375
  88.9 0.0 copy-start.1
  88.9 3.3 %copy.13 = bf16[1,512,2048]{2,1,0:T(8,128)(2,1)} copy(bf16[1,512,2048]{2,1,0:T(8,128)(2,1)} %get-tuple-element.6) | data formatting | bytes 4194304
  92.2 0.0 copy-done.1
  92.2 0.0 copy-start
  92.2 1.3 %copy.14 = bf16[1,512,2048]{2,1,0:T(8,128)(2,1)} copy(bf16[1,512,2048]{2,1,0:T(8,128)(2,1)S(1)} %copy-done.1) | data formatting | bytes 4194304
  93.6 1.0 %copy-done = bf16[1,512,2048]{2,1,0:T(8,128)(2,1)S(1)} copy-done((bf16[1,512,2048]{2,1,0:T(8,128)(2,1)S(1)}, bf16[1,512,2048]{2,1,0:T(8,128)(2,1)}, u32[]{:S(2)}) %copy-start) | copy-done | bytes 2097176
  94.6 1.3 %copy.15 = bf16[1,512,2048]{2,1,0:T(8,128)(2,1)} copy(bf16[1,512,2048]{2,1,0:T(8,128)(2,1)S(1)} %copy-done) | data formatting | bytes 4194304
Async XLA Ops:
  88.9 3.3 %copy-start.1 = (bf16[1,512,2048]{2,1,0:T(8,128)(2,1)S(1)}, bf16[1,512,2048]{2,1,0:T(8,128)(2,1)}, u32[]{:S(2)}) copy-start(bf16[1,512,2048]{2,1,0:T(8,128)(2,1)} %get-tuple-element.7) | copy-start | bytes 6291460
  92.2 2.3 %copy-start = (bf16[1,512,2048]{2,1,0:T(8,128)(2,1)S(1)}, bf16[1,512,2048]{2,1,0:T(8,128)(2,1)}, u32[]{:S(2)}) copy-start(bf16[1,512,2048]{2,1,0:T(8,128)(2,1)} %get-tuple-element.8) | copy-start | bytes 6291460

commit v2 on v1

--- a/solution.py
+++ b/solution.py
@@ -18,13 +18,17 @@
 WIDTH = 2048
 HEADS = 16
 MODEL = 3072
-CHUNKS = 6
-CW = 256
+CHUNKS = 12
+CW = 128
 BLOCKS = 32
 ROWS = 64
 FEATURES = 4096
 
 
+def mark(name):
+    pass
+
+
 def nn(a, b):
     return lax.dot_general(a, b, (((1,), (0,)), ((), ())), preferred_element_type=F32)
 
@@ -37,14 +41,19 @@
     return pl.ds(pl.multiple_of(h * HEAD, HEAD), HEAD)
 
 
+def place(c, part):
+    if c < CHUNKS - 2:
+        return c // 2 * 4 * CW + part * 2 * CW + c % 2 * CW
+    return (2 * c + part) * CW
+
+
 def kernel(
     q_hbm, k_hbm, v_hbm, up_hbm, w_hbm, gain_hbm, ld_hbm,
-    dq_hbm, dk_hbm, dv_hbm,
-    q, k, v, w, up, att, gh, ga, wqt, ccol, crow, mta, mtb,
-    own_f, got_f, scan_f, state, own_b, got_b, scan_b, later,
-    totals, tot_in, sq_own, sq_in, cr_own, cr_in, inv, fac, gain, ld,
-    dqs, dks, dvs,
-    load_sem, tot_sem, a2a_sem, perm_send, perm_recv, fwd_send, fwd_recv, tp_sem, out_sem,
+    dqs, att, gh, k, v, later, ccol, totals,
+    q, w, up, ga, wqt, crow, mta, mtb,
+    own_f, got_f, scan_f, state, own_b, got_b, scan_b,
+    tot_in, sq_own, sq_in, cr_own, cr_in, inv, fac, gain, ld,
+    load_sem, tot_sem, a2a_sem, perm_send, perm_recv, fwd_send, fwd_recv, tp_sem,
 ):
     z, y, x = (lax.axis_index(a) for a in SEQ)
     me = z * 8 + y * 2 + x
@@ -52,10 +61,14 @@
     sibling = {"tp": 1 - tp}
     across = {"pp": 1 - lax.axis_index("pp")}
 
+    def device_of(p):
+        return {"seq_0": p // 8, "seq_1": lax.rem(p // 2, 4), "seq_2": lax.rem(p, 2)}
+
     def peer(i):
         p = lax.rem(me + i, BLOCKS)
-        return p, {"seq_0": p // 8, "seq_1": lax.rem(p // 2, 4), "seq_2": lax.rem(p, 2)}
-
+        return p, device_of(p)
+
+    mark("loads")
     loads = []
 
     def load(src, dst):
@@ -70,13 +83,15 @@
     q_load = load(q_hbm.at[0], q)
     gain_load = load(gain_hbm, gain)
     w_loads = []
-    for j in range(CHUNKS):
+    for j in (0, 2, 4, 6, 8, 10, 11):
+        wide = CW if j >= CHUNKS - 2 else 2 * CW
         for part, side in enumerate((tp, 1 - tp)):
             at = pl.multiple_of(side * (MODEL // 2) + j * CW, CW)
             w_loads.append(
-                load(w_hbm.at[0, :, pl.ds(at, CW)], w.at[:, pl.ds((2 * j + part) * CW, CW)])
+                load(w_hbm.at[0, :, pl.ds(at, wide)], w.at[:, pl.ds(place(j, part), wide)])
             )
 
+    mark("barrier")
     barrier = pltpu.get_barrier_semaphore()
 
     @pl.loop(1, BLOCKS)
@@ -91,7 +106,7 @@
     def permute(j):
         return pltpu.make_async_remote_copy(
             src_ref=up_hbm.at[0, :, pl.ds(j * CW, CW)],
-            dst_ref=up.at[:, pl.ds(2 * j * CW, CW)],
+            dst_ref=up.at[:, pl.ds(place(j, 0), CW)],
             send_sem=perm_send.at[j],
             recv_sem=perm_recv.at[j],
             device_id=across,
@@ -100,8 +115,8 @@
 
     def forward(j):
         return pltpu.make_async_remote_copy(
-            src_ref=up.at[:, pl.ds(2 * j * CW, CW)],
-            dst_ref=up.at[:, pl.ds((2 * j + 1) * CW, CW)],
+            src_ref=up.at[:, pl.ds(place(j, 0), CW)],
+            dst_ref=up.at[:, pl.ds(place(j, 1), CW)],
             send_sem=fwd_send.at[j],
             recv_sem=fwd_recv.at[j],
             device_id=sibling,
@@ -127,31 +142,35 @@
         whole = ref.at[pl.ds(0, BLOCKS - 1)]
         pltpu.make_async_copy(whole, whole, sem).wait()
 
-    for j in (0, 1):
+    mark("perm01")
+    for j in (0, 1, 2):
         permute(j).start()
 
     ld_load.wait()
+    mark("cumsum")
     cum = ld[...]
-    place = lax.broadcasted_iota(jnp.int32, (HEADS, TOK), 1)
+    column_of = lax.broadcasted_iota(jnp.int32, (HEADS, TOK), 1)
     step = 1
     while step < TOK:
         moved = pltpu.roll(cum, step, 1)
-        cum = cum + jnp.where(place >= step, moved, 0.0)
+        cum = cum + jnp.where(column_of >= step, moved, 0.0)
         step *= 2
     crow[...] = cum
     total = jnp.broadcast_to(cum[:, TOK - 1 : TOK], (HEADS, HEAD))
     for h in range(HEADS):
         totals[2 * h : 2 * h + 1, 0] = total[h : h + 1]
         totals[2 * h + 1 : 2 * h + 2, 0] = total[h : h + 1]
-    exchange(totals, tot_in, tot_sem.at[0], tot_sem.at[1])
+    mark("ccol")
     turned = cum.T
     for h in range(HEADS):
         ccol[h] = jnp.broadcast_to(turned[:, h : h + 1], (TOK, HEAD))
 
+    mark("kvwait")
     k_load.wait()
     v_load.wait()
 
-    @pl.loop(0, HEADS)
+    mark("localstate")
+    @pl.loop(0, HEADS, unroll=4)
     def _(h):
         tail = jnp.exp(totals[2 * h] - ccol[h])
         weighted = (k[:, lanes(h)].astype(F32) * tail).astype(BF)
@@ -159,11 +178,14 @@
         own_f[2 * h] = local_state[:ROWS]
         own_f[2 * h + 1] = local_state[ROWS:]
 
+    mark("a2a_f1_send")
     exchange(own_f, got_f, a2a_sem.at[0], a2a_sem.at[1])
-    for j in (2, 3):
+    exchange(totals, tot_in, tot_sem.at[0], tot_sem.at[1])
+    for j in (3, 4, 5):
         permute(j).start()
     q_load.wait()
 
+    mark("intra")
     lower = lax.broadcasted_iota(jnp.int32, (HALF, HALF), 0) >= lax.broadcasted_iota(
         jnp.int32, (HALF, HALF), 1
     )
@@ -211,41 +233,65 @@
         wq = (qh.astype(F32) * jnp.exp(ccol[h])).astype(BF)
         wqt[h] = wq.T
 
+    mark("wait_f1")
     arrived(tot_in, tot_sem.at[1])
     arrived(got_f, a2a_sem.at[1])
+    mark("scan_f")
     running = jnp.zeros((ROWS, HEAD), F32)
     for b in range(BLOCKS):
         scan_f[b] = running.astype(BF)
         running = jnp.exp(tot_in[b]) * running + got_f[b].astype(F32)
+    mark("a2a_f2_send")
     exchange(scan_f, state, a2a_sem.at[2], a2a_sem.at[3])
-    for j in (4, 5):
+    for j in range(6, CHUNKS):
         permute(j).start()
 
+    mark("wload")
     gain_load.wait()
     for copy in w_loads:
         copy.wait()
 
-    def hidden(j, first):
+    def hidden(start, depth, first):
         @pl.loop(0, 4)
         def _(n):
             at = pl.ds(pl.multiple_of(n * 512, 512), 512)
-            part = nt(up[:, 2 * j * CW : (2 * j + 2) * CW], w[at, 2 * j * CW : (2 * j + 2) * CW])
+            part = nt(up[:, start : start + depth], w[at, start : start + depth])
             if first:
                 gh[:, at] = part
             else:
                 gh[:, at] += part
 
-    for j in (0, 1, 2):
-        permute(j).wait_recv()
-        forward(j).start()
-    for j in (0, 1):
-        forward(j).wait_recv()
-        hidden(j, j == 0)
-
+    def relay(*chunks):
+        for j in chunks:
+            permute(j).wait_recv()
+            forward(j).start()
+
+    def relayed(*chunks):
+        for j in chunks:
+            forward(j).wait_recv()
+
+    mark("relay012")
+    relay(0, 1, 2, 3)
+    relayed(0, 1)
+    mark("hidden01")
+    hidden(0, 512, True)
+    mark("relay4")
+    relay(4)
+    relayed(2, 3)
+    mark("hidden23")
+    hidden(512, 512, False)
+    mark("relay5")
+    relay(5)
+    relayed(4, 5)
+    mark("hidden45")
+    hidden(1024, 512, False)
+
+    mark("wait_f2")
     arrived(state, a2a_sem.at[3])
+    mark("att_inter")
     sq_own[...] = jnp.zeros_like(sq_own)
 
-    @pl.loop(0, HEADS)
+    @pl.loop(0, HEADS, unroll=4)
     def _(h):
         st = jnp.concatenate([state[2 * h], state[2 * h + 1]], axis=0)
         new = att[:, lanes(h)] + jnp.exp(ccol[h]) * nn(q[:, lanes(h)], st)
@@ -264,46 +310,71 @@
 
     squares = to_sibling(sq_own, sq_in, 0)
     squares.start()
-    for j in range(2, CHUNKS):
-        if j > 2:
-            permute(j).wait_recv()
-            forward(j).start()
-        forward(j).wait_recv()
-        hidden(j, False)
-        if j == 2:
-            squares.wait_recv()
-            square_total = jnp.sum(sq_own[...] + sq_in[...], axis=1, keepdims=True)
-            inv[...] = jnp.broadcast_to(
-                1.0 / jnp.sqrt(square_total / FEATURES + EPS), (TOK, HEAD)
-            )
-
+    mark("relay67")
+    relay(6, 7)
+    squares.wait_recv()
+    mark("inverse")
+    square_total = jnp.sum(sq_own[...] + sq_in[...], axis=1, keepdims=True)
+    inv[...] = jnp.broadcast_to(1.0 / jnp.sqrt(square_total / FEATURES + EPS), (TOK, HEAD))
+    relayed(6, 7)
+    mark("hidden67")
+    hidden(1536, 512, False)
+    mark("relay89")
+    relay(8, 9)
+    relayed(8, 9)
+    mark("hidden89")
+    hidden(2048, 512, False)
+    mark("relay10")
+    relay(10)
+    relayed(10)
+    mark("hidden10")
+    hidden(2560, 256, False)
+    mark("relay11")
+    relay(11)
     cr_own[...] = jnp.zeros_like(cr_own)
-
-    @pl.loop(0, HEADS)
-    def _(h):
-        norm = gh[:, lanes(h)] * gain[:, lanes(h)]
-        gh[:, lanes(h)] = norm
-        cr_own[...] += norm * att[:, lanes(h)]
+    relayed(11)
+    mark("hidden11")
+
+    @pl.loop(0, 4)
+    def _(n):
+        at = pl.ds(pl.multiple_of(n * 512, 512), 512)
+        norm = (gh[:, at] + nt(up[:, 2816:], w[at, 2816:])) * gain[:, at]
+        gh[:, at] = norm
+        both = norm * att[:, at]
+        cr_own[...] += (both[:, :128] + both[:, 128:256]) + (both[:, 256:384] + both[:, 384:])
 
     crossed = to_sibling(cr_own, cr_in, 1)
     crossed.start()
+    mark("cross_wait")
     crossed.wait_recv()
     cross_total = jnp.sum(cr_own[...] + cr_in[...], axis=1, keepdims=True)
     inverse = inv[...]
     fac[...] = inverse * inverse * inverse * jnp.broadcast_to(cross_total / FEATURES, (TOK, HEAD))
 
-    @pl.loop(0, HEADS)
-    def _(h):
+    mark("ga_passed")
+    @pl.loop(0, HEADS, unroll=2)
+    def _(i):
+        h = lax.rem(me // 2 + i, HEADS)
         grad = (inv[...] * gh[:, lanes(h)] - fac[...] * att[:, lanes(h)]).astype(BF)
         ga[:, lanes(h)] = grad
         passed = nn(wqt[h], grad).astype(BF)
         own_b[2 * h] = passed[:ROWS]
         own_b[2 * h + 1] = passed[ROWS:]
-
-    exchange(own_b, got_b, a2a_sem.at[4], a2a_sem.at[5])
-
-    def put(src, dst, h, i):
-        pltpu.make_async_copy(src.at[:, lanes(h)], dst.at[0, :, lanes(h)], out_sem.at[i]).start()
+        for side in (0, 1):
+            p = 2 * h + side
+
+            @pl.when(p != me)
+            def _():
+                pltpu.make_async_remote_copy(
+                    src_ref=own_b.at[p],
+                    dst_ref=got_b.at[me],
+                    send_sem=a2a_sem.at[4],
+                    recv_sem=a2a_sem.at[5],
+                    device_id=device_of(p),
+                    device_id_type=MESH,
+                ).start()
+
+    got_b[me] = own_b[me]
 
     def gradients(h):
         qh, kh, vh, gah = q[:, lanes(h)], k[:, lanes(h)], v[:, lanes(h)], ga[:, lanes(h)]
@@ -319,7 +390,6 @@
         inter = head * nt(gah, st)
         dqs[:HALF, lanes(h)] = (dq0 + inter[:HALF]).astype(BF)
         dqs[HALF:, lanes(h)] = (dq1 + inter[HALF:]).astype(BF)
-        put(dqs, dq_hbm, h, 0)
         t00, t01, t11 = turned_parts(h)
         n0 = jnp.concatenate(
             [(nt(v0, g0) * t00).astype(BF), (nt(v0, g1) * t01).astype(BF)], axis=1
@@ -330,30 +400,26 @@
         gh[:HALF, lanes(h)] = nn(mta[h], gah)
         gh[HALF:, lanes(h)] = nn(mtb[h], g1)
 
+    mark("grad1")
     pl.loop(0, HEADS // 2)(gradients)
 
+    mark("wait_b1")
     arrived(got_b, a2a_sem.at[5])
+    mark("scan_b")
     running = jnp.zeros((ROWS, HEAD), F32)
     for b in reversed(range(BLOCKS)):
         scan_b[b] = running.astype(BF)
         running = jnp.exp(tot_in[b]) * running + got_b[b].astype(F32)
+    mark("a2a_b2_send")
     exchange(scan_b, later, a2a_sem.at[6], a2a_sem.at[7])
 
+    mark("grad2")
     pl.loop(HEADS // 2, HEADS)(gradients)
 
+    mark("wait_b2")
     arrived(later, a2a_sem.at[7])
 
-    @pl.loop(0, HEADS)
-    def _(h):
-        lt = jnp.concatenate([later[2 * h], later[2 * h + 1]], axis=0)
-        tail = jnp.exp(totals[2 * h] - ccol[h])
-        dks[:, lanes(h)] = (att[:, lanes(h)] + tail * nt(v[:, lanes(h)], lt)).astype(BF)
-        put(dks, dk_hbm, h, 1)
-        dvs[:, lanes(h)] = (gh[:, lanes(h)] + tail * nn(k[:, lanes(h)], lt)).astype(BF)
-        put(dvs, dv_hbm, h, 2)
-
-    for i, (src, dst) in enumerate(((dqs, dq_hbm), (dks, dk_hbm), (dvs, dv_hbm))):
-        pltpu.make_async_copy(src, dst.at[0], out_sem.at[i]).wait()
+    mark("sendwaits")
     arrived(totals, tot_sem.at[0])
     for i, ref in enumerate((own_f, scan_f, own_b, scan_b)):
         arrived(ref, a2a_sem.at[2 * i])
@@ -362,50 +428,81 @@
         forward(j).wait_send()
     squares.wait_send()
     crossed.wait_send()
+    mark(None)
+
+
+def finish(
+    dqs, att, gh, k, v, later, ccol, totals, dq_hbm, dk_hbm, dv_hbm, dks, dvs, out_sem
+):
+    pltpu.make_async_copy(dqs, dq_hbm.at[0], out_sem.at[0]).start()
+
+    def put(src, dst, h, i):
+        pltpu.make_async_copy(src.at[:, lanes(h)], dst.at[0, :, lanes(h)], out_sem.at[i]).start()
+
+    @pl.loop(0, HEADS, unroll=2)
+    def _(h):
+        lt = jnp.concatenate([later[2 * h], later[2 * h + 1]], axis=0)
+        tail = jnp.exp(totals[2 * h] - ccol[h])
+        dks[:, lanes(h)] = (att[:, lanes(h)] + tail * nt(v[:, lanes(h)], lt)).astype(BF)
+        put(dks, dk_hbm, h, 1)
+        dvs[:, lanes(h)] = (gh[:, lanes(h)] + tail * nn(k[:, lanes(h)], lt)).astype(BF)
+        put(dvs, dv_hbm, h, 2)
+
+    for i, (src, dst) in enumerate(((dqs, dq_hbm), (dks, dk_hbm), (dvs, dv_hbm))):
+        pltpu.make_async_copy(src, dst.at[0], out_sem.at[i]).wait()
 
 
 def local(queries, keys, values, upstream, out_weight, gain, log_decay):
-    piece = pltpu.VMEM((BLOCKS, ROWS, HEAD), BF)
-    column = pltpu.VMEM((TOK, HEAD), F32)
-    rows_bf = pltpu.VMEM((TOK, WIDTH), BF)
-    rows_f32 = pltpu.VMEM((TOK, WIDTH), F32)
+    vmem = pltpu.VMEM
+    piece = vmem((BLOCKS, ROWS, HEAD), BF)
+    column = vmem((TOK, HEAD), F32)
+    rows_bf = vmem((TOK, WIDTH), BF)
+    rows_f32 = vmem((TOK, WIDTH), F32)
+    columns = vmem((HEADS, TOK, HEAD), F32)
+    totals = vmem((BLOCKS, 1, HEAD), F32)
     dma = pltpu.SemaphoreType.DMA
     hbm = pl.BlockSpec(memory_space=pl.ANY)
-    out = jax.ShapeDtypeStruct((1, TOK, WIDTH), BF)
-    return pl.pallas_call(
+    here = pl.BlockSpec(memory_space=vmem)
+    kept = pl.pallas_call(
         kernel,
-        out_shape=(out, out, out),
+        out_shape=(rows_bf, rows_f32, rows_f32, rows_bf, rows_bf, piece, columns, totals),
         in_specs=[hbm] * 7,
-        out_specs=[hbm] * 3,
+        out_specs=[here] * 8,
         scratch_shapes=[
-            rows_bf, rows_bf, rows_bf,
-            pltpu.VMEM((WIDTH, MODEL), BF),
-            pltpu.VMEM((TOK, MODEL), BF),
-            rows_f32, rows_f32, rows_bf,
-            pltpu.VMEM((HEADS, HEAD, TOK), BF),
-            pltpu.VMEM((HEADS, TOK, HEAD), F32),
-            pltpu.VMEM((HEADS, TOK), F32),
-            pltpu.VMEM((HEADS, HALF, TOK), BF),
-            pltpu.VMEM((HEADS, HALF, HALF), BF),
-            piece, piece, piece, piece, piece, piece, piece, piece,
-            pltpu.VMEM((BLOCKS, 1, HEAD), F32),
-            pltpu.VMEM((BLOCKS, 1, HEAD), F32),
+            rows_bf,
+            vmem((WIDTH, MODEL), BF),
+            vmem((TOK, MODEL), BF),
+            rows_bf,
+            vmem((HEADS, HEAD, TOK), BF),
+            vmem((HEADS, TOK), F32),
+            vmem((HEADS, HALF, TOK), BF),
+            vmem((HEADS, HALF, HALF), BF),
+            piece, piece, piece, piece, piece, piece, piece,
+            totals,
             column, column, column, column, column, column,
-            pltpu.VMEM((1, WIDTH), F32),
-            pltpu.VMEM((HEADS, TOK), F32),
-            rows_bf, rows_bf, rows_bf,
-            dma((5 + 2 * CHUNKS,)),
+            vmem((1, WIDTH), F32),
+            vmem((HEADS, TOK), F32),
+            dma((19,)),
             dma((2,)),
             dma((8,)),
             dma((CHUNKS,)), dma((CHUNKS,)), dma((CHUNKS,)), dma((CHUNKS,)),
             dma((4,)),
-            dma((3,)),
         ],
         compiler_params=pltpu.CompilerParams(
-            collective_id=0, has_side_effects=True, vmem_limit_bytes=67043328
+            collective_id=0, has_side_effects=True, vmem_limit_bytes=45 << 20
         ),
         name="decayed_backward",
     )(queries, keys, values, upstream, out_weight, gain, log_decay)
+    out = jax.ShapeDtypeStruct((1, TOK, WIDTH), BF)
+    return pl.pallas_call(
+        finish,
+        out_shape=(out, out, out),
+        in_specs=[here] * 8,
+        out_specs=[hbm] * 3,
+        scratch_shapes=[rows_bf, rows_bf, dma((3,))],
+        compiler_params=pltpu.CompilerParams(vmem_limit_bytes=24 << 20),
+        name="finish",
+    )(*kept)
 
 
 def solution(mesh):

time: 97.5 us -> 86.9 us (0.89); the launches traced: 95.9 us -> 86.8 us
  local copies, waits for them, and re-layouts: 6.98 us -> 0 us
  Pallas kernels: 88.3 us -> 86.1 us
    unnamed x7 -> x0, local copies, waits for them, and re-layouts: 6.98 us -> none
    pallas_call x1 -> x2, Pallas kernels: 88.3 us -> 86.1 us  [the longest x1 82.4 us: local(): pl.pallas_call(kernel, out_shape=(rows_bf, rows_f32, rows_f32, rows_bf, r...]
where the time goes in v2:
time: 86.9 us; the launch traced here: 86.8 us
  Pallas kernels  86.1 us (99%)
    pallas_call x1, Pallas kernels, local(): pl.pallas_call(kernel, out_shape=(rows_bf, rows_f32, rows_f32, rows_bf, r...  82.4 us
    pallas_call x1, Pallas kernels, local(): pl.pallas_call(finish, out_shape=(out, out, out), in_specs=[here] * 8, ou...  3.78 us

profile of v2, /device:TPU:1, one launch (start us, length us, event | category | flops | bytes accessed | tf_op | source)
XLA Modules:
  0.0 86.8 jit_solution(11403192666547502117)
XLA Ops:
  0.6 82.4 %decayed_backward.1 = (bf16[512,2048]{1,0:T(8,128)(2,1)S(1)}, f32[512,2048]{1,0:T(8,128)S(1)}, f32[512,2048]{1,0:T(8,128)S(1)}, bf16[512,2048]{1,0:T(8,128)(2,1)...) custom-call(bf16[1,512,2048]{2,1,0:T(8,128)(2,1)} %q_hbm.1, ...), custom_call_target="tpu_custom_call" | custom-call | tf_op jit(solution)/shard_map/decayed_backward/pallas_call | solution.py:466
  83.0 3.8 %finish.1 = (bf16[1,512,2048]{2,1,0:T(8,128)(2,1)}, bf16[1,512,2048]{2,1,0:T(8,128)(2,1)}, bf16[1,512,2048]{2,1,0:T(8,128)(2,1)}) custom-call(bf16[512,2048]{1,0:T(8,128)(2,1)S(1)} %get-tuple-element.11.dqs, f32[512,2048]{1,0:T(8,128)S(1)} %get-tuple-element.12.att, f32[512,2048]{1,0:T(8,128)S(1)} %get-tuple-element.13.gh, ...), custom_call_target="tpu_custom_call" | custom-call | tf_op jit(solution)/shard_map/finish/pallas_call | solution.py:497

commit v3 on v2

--- a/solution.py
+++ b/solution.py
@@ -41,6 +41,23 @@
     return pl.ds(pl.multiple_of(h * HEAD, HEAD), HEAD)
 
 
+def pair_lanes(i):
+    return pl.ds(pl.multiple_of(i * 2 * HEAD, 2 * HEAD), 2 * HEAD)
+
+
+def two_states(ref, i):
+    none = jnp.zeros((HEAD, HEAD), BF)
+    first = jnp.concatenate([ref[4 * i], ref[4 * i + 1]], axis=0)
+    second = jnp.concatenate([ref[4 * i + 2], ref[4 * i + 3]], axis=0)
+    return jnp.concatenate(
+        [jnp.concatenate([first, none], axis=1), jnp.concatenate([none, second], axis=1)], axis=0
+    )
+
+
+def two_columns(ref, i):
+    return jnp.concatenate([ref[2 * i], ref[2 * i + 1]], axis=1)
+
+
 def place(c, part):
     if c < CHUNKS - 2:
         return c // 2 * 4 * CW + part * 2 * CW + c % 2 * CW
@@ -52,8 +69,8 @@
     dqs, att, gh, k, v, later, ccol, totals,
     q, w, up, ga, wqt, crow, mta, mtb,
     own_f, got_f, scan_f, state, own_b, got_b, scan_b,
-    tot_in, sq_own, sq_in, cr_own, cr_in, inv, fac, gain, ld,
-    load_sem, tot_sem, a2a_sem, perm_send, perm_recv, fwd_send, fwd_recv, tp_sem,
+    tot_in, sq_own, sq_in, cr_own, cr_in, inv, fac, gain, ld, b_own, b_in,
+    load_sem, tot_sem, a2a_sem, perm_send, perm_recv, fwd_send, fwd_recv, tp_sem, b_sem,
 ):
     z, y, x = (lax.axis_index(a) for a in SEQ)
     me = z * 8 + y * 2 + x
@@ -64,9 +81,15 @@
     def device_of(p):
         return {"seq_0": p // 8, "seq_1": lax.rem(p // 2, 4), "seq_2": lax.rem(p, 2)}
 
-    def peer(i):
-        p = lax.rem(me + i, BLOCKS)
-        return p, device_of(p)
+    zs = [lax.rem(z + d, 4) for d in range(4)]
+    ys = [lax.rem(y + d, 4) for d in range(4)]
+    xs = [x, 1 - x]
+    peers = [
+        (zs[i] * 8 + ys[j] * 2 + xs[k], {"seq_0": zs[i], "seq_1": ys[j], "seq_2": xs[k]})
+        for i in range(4)
+        for j in range(4)
+        for k in range(2)
+    ][1:]
 
     mark("loads")
     loads = []
@@ -94,11 +117,8 @@
     mark("barrier")
     barrier = pltpu.get_barrier_semaphore()
 
-    @pl.loop(1, BLOCKS)
-    def _(i):
-        _, device = peer(i)
+    for _, device in peers:
         pl.semaphore_signal(barrier, inc=1, device_id=device, device_id_type=MESH)
-
     pl.semaphore_signal(barrier, inc=1, device_id=sibling, device_id_type=MESH)
     pl.semaphore_signal(barrier, inc=1, device_id=across, device_id_type=MESH)
     pl.semaphore_wait(barrier, BLOCKS + 1)
@@ -124,9 +144,7 @@
         )
 
     def exchange(src, dst, send_sem, recv_sem):
-        @pl.loop(1, BLOCKS)
-        def _(i):
-            p, device = peer(i)
+        for p, device in peers:
             pltpu.make_async_remote_copy(
                 src_ref=src.at[p],
                 dst_ref=dst.at[me],
@@ -135,7 +153,6 @@
                 device_id=device,
                 device_id_type=MESH,
             ).start()
-
         dst[me] = src[me]
 
     def arrived(ref, sem):
@@ -143,7 +160,7 @@
         pltpu.make_async_copy(whole, whole, sem).wait()
 
     mark("perm01")
-    for j in (0, 1, 2):
+    for j in (0, 1):
         permute(j).start()
 
     ld_load.wait()
@@ -181,7 +198,7 @@
     mark("a2a_f1_send")
     exchange(own_f, got_f, a2a_sem.at[0], a2a_sem.at[1])
     exchange(totals, tot_in, tot_sem.at[0], tot_sem.at[1])
-    for j in (3, 4, 5):
+    for j in (2, 3, 4):
         permute(j).start()
     q_load.wait()
 
@@ -243,7 +260,7 @@
         running = jnp.exp(tot_in[b]) * running + got_f[b].astype(F32)
     mark("a2a_f2_send")
     exchange(scan_f, state, a2a_sem.at[2], a2a_sem.at[3])
-    for j in range(6, CHUNKS):
+    for j in range(5, CHUNKS):
         permute(j).start()
 
     mark("wload")
@@ -275,28 +292,25 @@
     relayed(0, 1)
     mark("hidden01")
     hidden(0, 512, True)
-    mark("relay4")
+    mark("relay23")
     relay(4)
     relayed(2, 3)
     mark("hidden23")
     hidden(512, 512, False)
-    mark("relay5")
-    relay(5)
-    relayed(4, 5)
-    mark("hidden45")
-    hidden(1024, 512, False)
 
     mark("wait_f2")
     arrived(state, a2a_sem.at[3])
     mark("att_inter")
     sq_own[...] = jnp.zeros_like(sq_own)
 
-    @pl.loop(0, HEADS, unroll=4)
-    def _(h):
-        st = jnp.concatenate([state[2 * h], state[2 * h + 1]], axis=0)
-        new = att[:, lanes(h)] + jnp.exp(ccol[h]) * nn(q[:, lanes(h)], st)
-        att[:, lanes(h)] = new
-        sq_own[...] += new * new
+    @pl.loop(0, HEADS // 2, unroll=2)
+    def _(i):
+        at = pair_lanes(i)
+        new = att[:, at] + jnp.exp(two_columns(ccol, i)) * nn(q[:, at], two_states(state, i))
+        att[:, at] = new
+        ga[:, at] = (new * gain[:, at]).astype(BF)
+        both = new * new
+        sq_own[...] += both[:, :HEAD] + both[:, HEAD:]
 
     def to_sibling(src, dst, i):
         return pltpu.make_async_remote_copy(
@@ -308,14 +322,35 @@
             device_id_type=MESH,
         )
 
+    def tail_product():
+        b_own[...] = nn(ga[...], w[:, 2560:]).astype(BF)
+        for at in range(0, 4 * CW, CW):
+            copy = pltpu.make_async_remote_copy(
+                src_ref=b_own.at[:, pl.ds(at, CW)],
+                dst_ref=b_in.at[:, pl.ds(at + CW if at % (2 * CW) == 0 else at - CW, CW)],
+                send_sem=b_sem.at[0],
+                recv_sem=b_sem.at[1],
+                device_id=sibling,
+                device_id_type=MESH,
+            )
+            copy.start()
+
     squares = to_sibling(sq_own, sq_in, 0)
     squares.start()
+    cr_own[...] = jnp.zeros_like(cr_own)
+    mark("tail_product")
+    tail_product()
+    mark("relay45")
+    relay(5)
+    relayed(4, 5)
+    mark("hidden45")
+    hidden(1024, 512, False)
+    mark("inverse")
+    squares.wait_recv()
+    square_total = jnp.sum(sq_own[...] + sq_in[...], axis=1, keepdims=True)
+    inv[...] = jnp.broadcast_to(1.0 / jnp.sqrt(square_total / FEATURES + EPS), (TOK, HEAD))
     mark("relay67")
     relay(6, 7)
-    squares.wait_recv()
-    mark("inverse")
-    square_total = jnp.sum(sq_own[...] + sq_in[...], axis=1, keepdims=True)
-    inv[...] = jnp.broadcast_to(1.0 / jnp.sqrt(square_total / FEATURES + EPS), (TOK, HEAD))
     relayed(6, 7)
     mark("hidden67")
     hidden(1536, 512, False)
@@ -323,57 +358,81 @@
     relay(8, 9)
     relayed(8, 9)
     mark("hidden89")
-    hidden(2048, 512, False)
+
+    @pl.loop(0, 4)
+    def _(n):
+        at = pl.ds(pl.multiple_of(n * 512, 512), 512)
+        new = gh[:, at] + nt(up[:, 2048:2560], w[at, 2048:2560])
+        gh[:, at] = new
+        both = new * gain[:, at] * att[:, at]
+        cr_own[...] += (both[:, :128] + both[:, 128:256]) + (both[:, 256:384] + both[:, 384:])
+
+    crossed = to_sibling(cr_own, cr_in, 1)
+    crossed.start()
     mark("relay10")
     relay(10)
+    mark("wait_b_in")
+    pltpu.make_async_copy(b_in, b_in, b_sem.at[1]).wait()
+    mark("relayed10")
     relayed(10)
     mark("hidden10")
     hidden(2560, 256, False)
     mark("relay11")
+    crossed.wait_recv()
     relay(11)
-    cr_own[...] = jnp.zeros_like(cr_own)
     relayed(11)
-    mark("hidden11")
-
-    @pl.loop(0, 4)
-    def _(n):
-        at = pl.ds(pl.multiple_of(n * 512, 512), 512)
-        norm = (gh[:, at] + nt(up[:, 2816:], w[at, 2816:])) * gain[:, at]
-        gh[:, at] = norm
-        both = norm * att[:, at]
-        cr_own[...] += (both[:, :128] + both[:, 128:256]) + (both[:, 256:384] + both[:, 384:])
-
-    crossed = to_sibling(cr_own, cr_in, 1)
-    crossed.start()
-    mark("cross_wait")
-    crossed.wait_recv()
-    cross_total = jnp.sum(cr_own[...] + cr_in[...], axis=1, keepdims=True)
+    mark("crossing11")
+    part = cr_own[...] + cr_in[...]
+    for at in range(0, 4 * CW, CW):
+        both = b_own[:, at : at + CW].astype(F32) + b_in[:, at : at + CW].astype(F32)
+        part += up[:, 2560 + at : 2560 + at + CW].astype(F32) * both
+    cross_total = jnp.sum(part, axis=1, keepdims=True)
     inverse = inv[...]
     fac[...] = inverse * inverse * inverse * jnp.broadcast_to(cross_total / FEATURES, (TOK, HEAD))
 
     mark("ga_passed")
-    @pl.loop(0, HEADS, unroll=2)
-    def _(i):
-        h = lax.rem(me // 2 + i, HEADS)
-        grad = (inv[...] * gh[:, lanes(h)] - fac[...] * att[:, lanes(h)]).astype(BF)
-        ga[:, lanes(h)] = grad
-        passed = nn(wqt[h], grad).astype(BF)
-        own_b[2 * h] = passed[:ROWS]
-        own_b[2 * h + 1] = passed[ROWS:]
-        for side in (0, 1):
-            p = 2 * h + side
-
-            @pl.when(p != me)
-            def _():
-                pltpu.make_async_remote_copy(
-                    src_ref=own_b.at[p],
-                    dst_ref=got_b.at[me],
-                    send_sem=a2a_sem.at[4],
-                    recv_sem=a2a_sem.at[5],
-                    device_id=device_of(p),
-                    device_id_type=MESH,
-                ).start()
-
+    low_rows, high_rows = pl.ds(0, ROWS // 2), pl.ds(ROWS // 2, ROWS // 2)
+
+    def send_piece(src, dst, p, device, rows, sem):
+        pltpu.make_async_remote_copy(
+            src_ref=src.at[p, rows],
+            dst_ref=dst.at[me, rows],
+            send_sem=a2a_sem.at[sem],
+            recv_sem=a2a_sem.at[sem + 1],
+            device_id=device,
+            device_id_type=MESH,
+        ).start()
+
+    def piece_arrived(ref, rows, sem):
+        whole = ref.at[pl.ds(0, BLOCKS - 1), rows]
+        pltpu.make_async_copy(whole, whole, a2a_sem.at[sem]).wait()
+
+    groups = [lax.rem(me // 8 + n, 4) for n in range(4)]
+
+    def normed(n):
+        at = pl.ds(pl.multiple_of(groups[n] * 512, 512), 512)
+        return (gh[:, at] + nt(up[:, 2816:], w[at, 2816:])) * gain[:, at]
+
+    norm = normed(0)
+    for n in range(4):
+        g = groups[n]
+        after = normed(n + 1) if n < 3 else None
+        for j in range(4):
+            h = 4 * g + j
+            grad = inv[...] * norm[:, j * HEAD : (j + 1) * HEAD] - fac[...] * att[:, lanes(h)]
+            grad = grad.astype(BF)
+            ga[:, lanes(h)] = grad
+            passed = nn(wqt[h], grad).astype(BF)
+            own_b[2 * h] = passed[:ROWS]
+            own_b[2 * h + 1] = passed[ROWS:]
+        for s in range(8):
+            if n > 0 or s > 0:
+                p = 8 * g + lax.rem(me + s, 8)
+                send_piece(own_b, got_b, p, device_of(p), low_rows, 4)
+        norm = after
+    mark("send_high")
+    for p, device in peers:
+        send_piece(own_b, got_b, p, device, high_rows, 6)
     got_b[me] = own_b[me]
 
     def gradients(h):
@@ -400,29 +459,41 @@
         gh[:HALF, lanes(h)] = nn(mta[h], gah)
         gh[HALF:, lanes(h)] = nn(mtb[h], g1)
 
+    def scan_back(rows):
+        running = jnp.zeros((ROWS // 2, HEAD), F32)
+        for b in reversed(range(BLOCKS)):
+            scan_b[b, rows] = running.astype(BF)
+            running = jnp.exp(tot_in[b]) * running + got_b[b, rows].astype(F32)
+        for p, device in peers:
+            send_piece(scan_b, later, p, device, rows, 8 if rows is low_rows else 10)
+        later[me, rows] = scan_b[me, rows]
+
     mark("grad1")
-    pl.loop(0, HEADS // 2)(gradients)
-
-    mark("wait_b1")
-    arrived(got_b, a2a_sem.at[5])
-    mark("scan_b")
-    running = jnp.zeros((ROWS, HEAD), F32)
-    for b in reversed(range(BLOCKS)):
-        scan_b[b] = running.astype(BF)
-        running = jnp.exp(tot_in[b]) * running + got_b[b].astype(F32)
-    mark("a2a_b2_send")
-    exchange(scan_b, later, a2a_sem.at[6], a2a_sem.at[7])
-
+    pl.loop(0, 4)(gradients)
+    mark("wait_b1a")
+    piece_arrived(got_b, low_rows, 5)
+    mark("scan_ba")
+    scan_back(low_rows)
     mark("grad2")
-    pl.loop(HEADS // 2, HEADS)(gradients)
-
+    pl.loop(4, 7)(gradients)
+    mark("wait_b1b")
+    piece_arrived(got_b, high_rows, 7)
+    mark("scan_bb")
+    scan_back(high_rows)
+    mark("grad3")
+    pl.loop(7, HEADS)(gradients)
     mark("wait_b2")
-    arrived(later, a2a_sem.at[7])
+    piece_arrived(later, low_rows, 9)
+    piece_arrived(later, high_rows, 11)
 
     mark("sendwaits")
     arrived(totals, tot_sem.at[0])
-    for i, ref in enumerate((own_f, scan_f, own_b, scan_b)):
-        arrived(ref, a2a_sem.at[2 * i])
+    arrived(own_f, a2a_sem.at[0])
+    arrived(scan_f, a2a_sem.at[2])
+    for rows, sem in ((low_rows, 4), (high_rows, 6)):
+        piece_arrived(own_b, rows, sem)
+        piece_arrived(scan_b, rows, sem + 4)
+    pltpu.make_async_copy(b_own, b_own, b_sem.at[0]).wait()
     for j in range(CHUNKS):
         permute(j).wait_send()
         forward(j).wait_send()
@@ -436,17 +507,19 @@
 ):
     pltpu.make_async_copy(dqs, dq_hbm.at[0], out_sem.at[0]).start()
 
-    def put(src, dst, h, i):
-        pltpu.make_async_copy(src.at[:, lanes(h)], dst.at[0, :, lanes(h)], out_sem.at[i]).start()
-
-    @pl.loop(0, HEADS, unroll=2)
-    def _(h):
-        lt = jnp.concatenate([later[2 * h], later[2 * h + 1]], axis=0)
-        tail = jnp.exp(totals[2 * h] - ccol[h])
-        dks[:, lanes(h)] = (att[:, lanes(h)] + tail * nt(v[:, lanes(h)], lt)).astype(BF)
-        put(dks, dk_hbm, h, 1)
-        dvs[:, lanes(h)] = (gh[:, lanes(h)] + tail * nn(k[:, lanes(h)], lt)).astype(BF)
-        put(dvs, dv_hbm, h, 2)
+    def put(src, dst, at, i):
+        pltpu.make_async_copy(src.at[:, at], dst.at[0, :, at], out_sem.at[i]).start()
+
+    @pl.loop(0, HEADS // 2, unroll=2)
+    def _(i):
+        at = pair_lanes(i)
+        lt = two_states(later, i)
+        total = jnp.concatenate([totals[4 * i], totals[4 * i + 2]], axis=1)
+        tail = jnp.exp(total - two_columns(ccol, i))
+        dks[:, at] = (att[:, at] + tail * nt(v[:, at], lt)).astype(BF)
+        put(dks, dk_hbm, at, 1)
+        dvs[:, at] = (gh[:, at] + tail * nn(k[:, at], lt)).astype(BF)
+        put(dvs, dv_hbm, at, 2)
 
     for i, (src, dst) in enumerate(((dqs, dq_hbm), (dks, dk_hbm), (dvs, dv_hbm))):
         pltpu.make_async_copy(src, dst.at[0], out_sem.at[i]).wait()
@@ -482,11 +555,14 @@
             column, column, column, column, column, column,
             vmem((1, WIDTH), F32),
             vmem((HEADS, TOK), F32),
+            vmem((TOK, 4 * CW), BF),
+            vmem((TOK, 4 * CW), BF),
             dma((19,)),
             dma((2,)),
-            dma((8,)),
+            dma((12,)),
             dma((CHUNKS,)), dma((CHUNKS,)), dma((CHUNKS,)), dma((CHUNKS,)),
             dma((4,)),
+            dma((2,)),
         ],
         compiler_params=pltpu.CompilerParams(
             collective_id=0, has_side_effects=True, vmem_limit_bytes=45 << 20

time: 86.9 us -> 84.1 us (0.968)
  Pallas kernels: 86.1 us -> 83.4 us
    pallas_call x1, Pallas kernels: 82.4 us -> 80.3 us  [local(): pl.pallas_call(kernel, out_shape=(rows_bf, rows_f32, rows_f32, rows_bf, r...]
where the time goes in v3:
time: 84.1 us; the launch traced here: 84 us
  Pallas kernels  83.4 us (99%)
    pallas_call x1, Pallas kernels, local(): pl.pallas_call(kernel, out_shape=(rows_bf, rows_f32, rows_f32, rows_bf, r...  80.3 us
    pallas_call x1, Pallas kernels, local(): pl.pallas_call(finish, out_shape=(out, out, out), in_specs=[here] * 8, ou...  3.08 us

profile of v3, /device:TPU:1, one launch (start us, length us, event | category | flops | bytes accessed | tf_op | source)
XLA Modules:
  0.0 84.0 jit_solution(18169819817238785551)
XLA Ops:
  0.6 80.3 %decayed_backward.1 = (bf16[512,2048]{1,0:T(8,128)(2,1)S(1)}, f32[512,2048]{1,0:T(8,128)S(1)}, f32[512,2048]{1,0:T(8,128)S(1)}, bf16[512,2048]{1,0:T(8,128)(2,1)...) custom-call(bf16[1,512,2048]{2,1,0:T(8,128)(2,1)} %q_hbm.1, ...), custom_call_target="tpu_custom_call" | custom-call | tf_op jit(solution)/shard_map/decayed_backward/pallas_call | solution.py:539
  81.0 3.1 %finish.1 = (bf16[1,512,2048]{2,1,0:T(8,128)(2,1)}, bf16[1,512,2048]{2,1,0:T(8,128)(2,1)}, bf16[1,512,2048]{2,1,0:T(8,128)(2,1)}) custom-call(bf16[512,2048]{1,0:T(8,128)(2,1)S(1)} %get-tuple-element.11.dqs, f32[512,2048]{1,0:T(8,128)S(1)} %get-tuple-element.12.att, f32[512,2048]{1,0:T(8,128)S(1)} %get-tuple-element.13.gh, ...), custom_call_target="tpu_custom_call" | custom-call | tf_op jit(solution)/shard_map/finish/pallas_call | solution.py:573

commit v4 on v3

--- a/solution.py
+++ b/solution.py
@@ -66,10 +66,10 @@
 
 def kernel(
     q_hbm, k_hbm, v_hbm, up_hbm, w_hbm, gain_hbm, ld_hbm,
-    dqs, att, gh, k, v, later, ccol, totals,
-    q, w, up, ga, wqt, crow, mta, mtb,
+    dqs, att, gh, k, v, later, tails,
+    ccol, totals, q, w, up, ga, wqt, crow, mta, mtb,
     own_f, got_f, scan_f, state, own_b, got_b, scan_b,
-    tot_in, sq_own, sq_in, cr_own, cr_in, inv, fac, gain, ld, b_own, b_in,
+    tot_in, sq_own, sq_in, cr_own, cr_in, inv, fac, gain, ld, b_own, b_in, w_last,
     load_sem, tot_sem, a2a_sem, perm_send, perm_recv, fwd_send, fwd_recv, tp_sem, b_sem,
 ):
     z, y, x = (lax.axis_index(a) for a in SEQ)
@@ -77,9 +77,6 @@
     tp = lax.axis_index("tp")
     sibling = {"tp": 1 - tp}
     across = {"pp": 1 - lax.axis_index("pp")}
-
-    def device_of(p):
-        return {"seq_0": p // 8, "seq_1": lax.rem(p // 2, 4), "seq_2": lax.rem(p, 2)}
 
     zs = [lax.rem(z + d, 4) for d in range(4)]
     ys = [lax.rem(y + d, 4) for d in range(4)]
@@ -190,6 +187,7 @@
     @pl.loop(0, HEADS, unroll=4)
     def _(h):
         tail = jnp.exp(totals[2 * h] - ccol[h])
+        tails[h] = tail
         weighted = (k[:, lanes(h)].astype(F32) * tail).astype(BF)
         local_state = nn(weighted.T, v[:, lanes(h)]).astype(BF)
         own_f[2 * h] = local_state[:ROWS]
@@ -286,6 +284,11 @@
     def relayed(*chunks):
         for j in chunks:
             forward(j).wait_recv()
+
+    @pl.loop(0, HEADS)
+    def _(h):
+        scale = jnp.broadcast_to(gain[:, lanes(h)], (HEAD, HEAD)).T
+        w_last[lanes(h), :] = (w[lanes(h), MODEL - CW :].astype(F32) * scale).astype(BF)
 
     mark("relay012")
     relay(0, 1, 2, 3)
@@ -371,24 +374,37 @@
     crossed.start()
     mark("relay10")
     relay(10)
-    mark("wait_b_in")
+    mark("own10")
+    hidden(2560, 128, False)
     pltpu.make_async_copy(b_in, b_in, b_sem.at[1]).wait()
-    mark("relayed10")
+    crossed.wait_recv()
+    mark("relay11")
+    relay(11)
     relayed(10)
-    mark("hidden10")
-    hidden(2560, 256, False)
-    mark("relay11")
-    crossed.wait_recv()
-    relay(11)
+    mark("sib10own11")
+
+    @pl.loop(0, 4)
+    def _(n):
+        at = pl.ds(pl.multiple_of(n * 512, 512), 512)
+        new = gh[:, at] + nt(up[:, 2688:2944], w[at, 2688:2944])
+        inverse = inv[...]
+        gh[:, at] = new * gain[:, at] * jnp.concatenate([inverse] * 4, axis=1)
+
+    crossed.wait_send()
+    part = cr_own[...] + cr_in[...]
+    for at in range(0, 3 * CW, CW):
+        both = b_own[:, at : at + CW].astype(F32) + b_in[:, at : at + CW].astype(F32)
+        part += up[:, 2560 + at : 2560 + at + CW].astype(F32) * both
+    cr_own[...] = part
+    mark("relayed11")
     relayed(11)
     mark("crossing11")
-    part = cr_own[...] + cr_in[...]
-    for at in range(0, 4 * CW, CW):
-        both = b_own[:, at : at + CW].astype(F32) + b_in[:, at : at + CW].astype(F32)
-        part += up[:, 2560 + at : 2560 + at + CW].astype(F32) * both
+    both = b_own[:, 3 * CW :].astype(F32) + b_in[:, 3 * CW :].astype(F32)
+    part = cr_own[...] + up[:, MODEL - CW :].astype(F32) * both
     cross_total = jnp.sum(part, axis=1, keepdims=True)
     inverse = inv[...]
     fac[...] = inverse * inverse * inverse * jnp.broadcast_to(cross_total / FEATURES, (TOK, HEAD))
+    up_last = (up[:, MODEL - CW :].astype(F32) * inverse).astype(BF)
 
     mark("ga_passed")
     low_rows, high_rows = pl.ds(0, ROWS // 2), pl.ds(ROWS // 2, ROWS // 2)
@@ -407,57 +423,63 @@
         whole = ref.at[pl.ds(0, BLOCKS - 1), rows]
         pltpu.make_async_copy(whole, whole, a2a_sem.at[sem]).wait()
 
-    groups = [lax.rem(me // 8 + n, 4) for n in range(4)]
-
-    def normed(n):
-        at = pl.ds(pl.multiple_of(groups[n] * 512, 512), 512)
-        return (gh[:, at] + nt(up[:, 2816:], w[at, 2816:])) * gain[:, at]
-
-    norm = normed(0)
-    for n in range(4):
-        g = groups[n]
-        after = normed(n + 1) if n < 3 else None
+    def last_step(n):
+        at = pl.ds(pl.multiple_of(zs[n] * 512, 512), 512)
+        gh[:, at] += nt(up_last, w_last[at, :])
+
+    def passing(n):
         for j in range(4):
-            h = 4 * g + j
-            grad = inv[...] * norm[:, j * HEAD : (j + 1) * HEAD] - fac[...] * att[:, lanes(h)]
-            grad = grad.astype(BF)
+            h = 4 * zs[n] + j
+            grad = (gh[:, lanes(h)] - fac[...] * att[:, lanes(h)]).astype(BF)
             ga[:, lanes(h)] = grad
             passed = nn(wqt[h], grad).astype(BF)
             own_b[2 * h] = passed[:ROWS]
             own_b[2 * h + 1] = passed[ROWS:]
-        for s in range(8):
-            if n > 0 or s > 0:
-                p = 8 * g + lax.rem(me + s, 8)
-                send_piece(own_b, got_b, p, device_of(p), low_rows, 4)
-        norm = after
+
+    def send_low(part):
+        for p, device in part:
+            send_piece(own_b, got_b, p, device, low_rows, 4)
+
+    last_step(0)
+    last_step(1)
+    passing(0)
+    passing(1)
+    last_step(2)
+    last_step(3)
+    send_low(peers[:15])
+    passing(2)
+    passing(3)
+    send_low(peers[15:])
     mark("send_high")
     for p, device in peers:
         send_piece(own_b, got_b, p, device, high_rows, 6)
     got_b[me] = own_b[me]
 
-    def gradients(h):
-        qh, kh, vh, gah = q[:, lanes(h)], k[:, lanes(h)], v[:, lanes(h)], ga[:, lanes(h)]
-        v0, v1, g0, g1 = vh[:HALF], vh[HALF:], gah[:HALF], gah[HALF:]
-        d00, d10, d11 = decay_parts(h)
-        m00 = (nt(g0, v0) * d00).astype(BF)
-        m10 = (nt(g1, v0) * d10).astype(BF)
-        m11 = (nt(g1, v1) * d11).astype(BF)
-        st = jnp.concatenate([state[2 * h], state[2 * h + 1]], axis=0)
-        head = jnp.exp(ccol[h])
-        dq0 = nn(m00, kh[:HALF])
-        dq1 = nn(jnp.concatenate([m10, m11], axis=1), kh)
-        inter = head * nt(gah, st)
-        dqs[:HALF, lanes(h)] = (dq0 + inter[:HALF]).astype(BF)
-        dqs[HALF:, lanes(h)] = (dq1 + inter[HALF:]).astype(BF)
-        t00, t01, t11 = turned_parts(h)
-        n0 = jnp.concatenate(
-            [(nt(v0, g0) * t00).astype(BF), (nt(v0, g1) * t01).astype(BF)], axis=1
-        )
-        n1 = (nt(v1, g1) * t11).astype(BF)
-        att[:HALF, lanes(h)] = nn(n0, qh)
-        att[HALF:, lanes(h)] = nn(n1, qh[HALF:])
-        gh[:HALF, lanes(h)] = nn(mta[h], gah)
-        gh[HALF:, lanes(h)] = nn(mtb[h], g1)
+    def gradients(i):
+        two = pair_lanes(i)
+        inter = jnp.exp(two_columns(ccol, i)) * nt(ga[:, two], two_states(state, i))
+        for side in (0, 1):
+            h = 2 * i + side
+            qh, kh, vh, gah = q[:, lanes(h)], k[:, lanes(h)], v[:, lanes(h)], ga[:, lanes(h)]
+            v0, v1, g0, g1 = vh[:HALF], vh[HALF:], gah[:HALF], gah[HALF:]
+            d00, d10, d11 = decay_parts(h)
+            m00 = (nt(g0, v0) * d00).astype(BF)
+            m10 = (nt(g1, v0) * d10).astype(BF)
+            m11 = (nt(g1, v1) * d11).astype(BF)
+            dq0 = nn(m00, kh[:HALF])
+            dq1 = nn(jnp.concatenate([m10, m11], axis=1), kh)
+            more = inter[:, side * HEAD : (side + 1) * HEAD]
+            dqs[:HALF, lanes(h)] = (dq0 + more[:HALF]).astype(BF)
+            dqs[HALF:, lanes(h)] = (dq1 + more[HALF:]).astype(BF)
+            t00, t01, t11 = turned_parts(h)
+            n0 = jnp.concatenate(
+                [(nt(v0, g0) * t00).astype(BF), (nt(v0, g1) * t01).astype(BF)], axis=1
+            )
+            n1 = (nt(v1, g1) * t11).astype(BF)
+            att[:HALF, lanes(h)] = nn(n0, qh)
+            att[HALF:, lanes(h)] = nn(n1, qh[HALF:])
+            gh[:HALF, lanes(h)] = nn(mta[h], gah)
+            gh[HALF:, lanes(h)] = nn(mtb[h], g1)
 
     def scan_back(rows):
         running = jnp.zeros((ROWS // 2, HEAD), F32)
@@ -469,19 +491,19 @@
         later[me, rows] = scan_b[me, rows]
 
     mark("grad1")
-    pl.loop(0, 4)(gradients)
+    pl.loop(0, 3)(gradients)
     mark("wait_b1a")
     piece_arrived(got_b, low_rows, 5)
     mark("scan_ba")
     scan_back(low_rows)
     mark("grad2")
-    pl.loop(4, 7)(gradients)
+    pl.loop(3, 5)(gradients)
     mark("wait_b1b")
     piece_arrived(got_b, high_rows, 7)
     mark("scan_bb")
     scan_back(high_rows)
     mark("grad3")
-    pl.loop(7, HEADS)(gradients)
+    pl.loop(5, HEADS // 2)(gradients)
     mark("wait_b2")
     piece_arrived(later, low_rows, 9)
     piece_arrived(later, high_rows, 11)
@@ -498,28 +520,28 @@
         permute(j).wait_send()
         forward(j).wait_send()
     squares.wait_send()
-    crossed.wait_send()
     mark(None)
 
 
 def finish(
-    dqs, att, gh, k, v, later, ccol, totals, dq_hbm, dk_hbm, dv_hbm, dks, dvs, out_sem
+    dqs, att, gh, k, v, later, tails, dq_hbm, dk_hbm, dv_hbm, dks, dvs, out_sem
 ):
     pltpu.make_async_copy(dqs, dq_hbm.at[0], out_sem.at[0]).start()
 
     def put(src, dst, at, i):
         pltpu.make_async_copy(src.at[:, at], dst.at[0, :, at], out_sem.at[i]).start()
 
-    @pl.loop(0, HEADS // 2, unroll=2)
-    def _(i):
-        at = pair_lanes(i)
-        lt = two_states(later, i)
-        total = jnp.concatenate([totals[4 * i], totals[4 * i + 2]], axis=1)
-        tail = jnp.exp(total - two_columns(ccol, i))
-        dks[:, at] = (att[:, at] + tail * nt(v[:, at], lt)).astype(BF)
-        put(dks, dk_hbm, at, 1)
-        dvs[:, at] = (gh[:, at] + tail * nn(k[:, at], lt)).astype(BF)
-        put(dvs, dv_hbm, at, 2)
+    @pl.loop(0, HEADS // 4)
+    def _(n):
+        for i in (2 * n, 2 * n + 1):
+            at = pair_lanes(i)
+            lt = two_states(later, i)
+            tail = two_columns(tails, i)
+            dks[:, at] = (att[:, at] + tail * nt(v[:, at], lt)).astype(BF)
+            dvs[:, at] = (gh[:, at] + tail * nn(k[:, at], lt)).astype(BF)
+        four = pl.ds(pl.multiple_of(n * 512, 512), 512)
+        put(dks, dk_hbm, four, 1)
+        put(dvs, dv_hbm, four, 2)
 
     for i, (src, dst) in enumerate(((dqs, dq_hbm), (dks, dk_hbm), (dvs, dv_hbm))):
         pltpu.make_async_copy(src, dst.at[0], out_sem.at[i]).wait()
@@ -538,10 +560,12 @@
     here = pl.BlockSpec(memory_space=vmem)
     kept = pl.pallas_call(
         kernel,
-        out_shape=(rows_bf, rows_f32, rows_f32, rows_bf, rows_bf, piece, columns, totals),
+        out_shape=(rows_bf, rows_f32, rows_f32, rows_bf, rows_bf, piece, columns),
         in_specs=[hbm] * 7,
-        out_specs=[here] * 8,
+        out_specs=[here] * 7,
         scratch_shapes=[
+            columns,
+            totals,
             rows_bf,
             vmem((WIDTH, MODEL), BF),
             vmem((TOK, MODEL), BF),
@@ -557,6 +581,7 @@
             vmem((HEADS, TOK), F32),
             vmem((TOK, 4 * CW), BF),
             vmem((TOK, 4 * CW), BF),
+            vmem((WIDTH, CW), BF),
             dma((19,)),
             dma((2,)),
             dma((12,)),
@@ -573,7 +598,7 @@
     return pl.pallas_call(
         finish,
         out_shape=(out, out, out),
-        in_specs=[here] * 8,
+        in_specs=[here] * 7,
         out_specs=[hbm] * 3,
         scratch_shapes=[rows_bf, rows_bf, dma((3,))],
         compiler_params=pltpu.CompilerParams(vmem_limit_bytes=24 << 20),

time: 84.1 us -> 80.3 us (0.955)
  Pallas kernels: 83.4 us -> 79.1 us
    pallas_call x1, Pallas kernels: 80.3 us -> 76.1 us  [local(): pl.pallas_call(kernel, out_shape=(rows_bf, rows_f32, rows_f32, rows_bf, r...]
where the time goes in v4:
time: 80.3 us; the launch traced here: 79.7 us
  Pallas kernels  79.1 us (99%)
    pallas_call x1, Pallas kernels, local(): pl.pallas_call(kernel, out_shape=(rows_bf, rows_f32, rows_f32, rows_bf, r...  76.1 us
    pallas_call x1, Pallas kernels, local(): pl.pallas_call(finish, out_shape=(out, out, out), in_specs=[here] * 7, ou...  2.99 us

profile of v4, /device:TPU:1, one launch (start us, length us, event | category | flops | bytes accessed | tf_op | source)
XLA Modules:
  0.0 79.7 jit_solution(14201410975960502786)
XLA Ops:
  0.6 76.1 %decayed_backward.1 = (bf16[512,2048]{1,0:T(8,128)(2,1)S(1)}, f32[512,2048]{1,0:T(8,128)S(1)}, f32[512,2048]{1,0:T(8,128)S(1)}, bf16[512,2048]{1,0:T(8,128)(2,1)...) custom-call(bf16[1,512,2048]{2,1,0:T(8,128)(2,1)} %q_hbm.1, ...), custom_call_target="tpu_custom_call" | custom-call | tf_op jit(solution)/shard_map/decayed_backward/pallas_call | solution.py:561
  76.7 3.0 %finish.1 = (bf16[1,512,2048]{2,1,0:T(8,128)(2,1)}, bf16[1,512,2048]{2,1,0:T(8,128)(2,1)}, bf16[1,512,2048]{2,1,0:T(8,128)(2,1)}) custom-call(bf16[512,2048]{1,0:T(8,128)(2,1)S(1)} %get-tuple-element.10.dqs, f32[512,2048]{1,0:T(8,128)S(1)} %get-tuple-element.11.att, f32[512,2048]{1,0:T(8,128)S(1)} %get-tuple-element.12.gh, ...), custom_call_target="tpu_custom_call" | custom-call | tf_op jit(solution)/shard_map/finish/pallas_call | solution.py:598

commit v5 on v4

--- a/solution.py
+++ b/solution.py
@@ -42,6 +42,8 @@
 
 
 def pair_lanes(i):
+    if isinstance(i, int):
+        return pl.ds(i * 2 * HEAD, 2 * HEAD)
     return pl.ds(pl.multiple_of(i * 2 * HEAD, 2 * HEAD), 2 * HEAD)
 
 
@@ -69,7 +71,7 @@
     dqs, att, gh, k, v, later, tails,
     ccol, totals, q, w, up, ga, wqt, crow, mta, mtb,
     own_f, got_f, scan_f, state, own_b, got_b, scan_b,
-    tot_in, sq_own, sq_in, cr_own, cr_in, inv, fac, gain, ld, b_own, b_in, w_last,
+    tot_in, sq_own, sq_in, cr_own, cr_in, inv, fac, gain, ld, b_own, b_in, w_last, up_from,
     load_sem, tot_sem, a2a_sem, perm_send, perm_recv, fwd_send, fwd_recv, tp_sem, b_sem,
 ):
     z, y, x = (lax.axis_index(a) for a in SEQ)
@@ -81,12 +83,18 @@
     zs = [lax.rem(z + d, 4) for d in range(4)]
     ys = [lax.rem(y + d, 4) for d in range(4)]
     xs = [x, 1 - x]
-    peers = [
-        (zs[i] * 8 + ys[j] * 2 + xs[k], {"seq_0": zs[i], "seq_1": ys[j], "seq_2": xs[k]})
-        for i in range(4)
-        for j in range(4)
-        for k in range(2)
-    ][1:]
+    def hops(at):
+        return min(at[0], 4 - at[0]) + min(at[1], 4 - at[1]) + at[2]
+
+    offsets = [(i, j, k) for i in range(4) for j in range(4) for k in range(2)][1:]
+    offsets.sort(key=hops, reverse=True)
+
+    def peer(at):
+        i, j, k = at
+        device = {"seq_0": zs[i], "seq_1": ys[j], "seq_2": xs[k]}
+        return zs[i] * 8 + ys[j] * 2 + xs[k], device
+
+    peers = [peer(at) for at in offsets]
 
     mark("loads")
     loads = []
@@ -97,6 +105,8 @@
         loads.append(copy)
         return copy
 
+    first, rest = pl.ds(0, 2 * CW), pl.ds(2 * CW, MODEL // 2 - 2 * CW)
+    up_loads = [load(up_hbm.at[0, :, cols], up_from.at[:, cols]) for cols in (first, rest)]
     ld_load = load(ld_hbm.at[0], ld)
     k_load = load(k_hbm.at[0], k)
     v_load = load(v_hbm.at[0], v)
@@ -122,7 +132,7 @@
 
     def permute(j):
         return pltpu.make_async_remote_copy(
-            src_ref=up_hbm.at[0, :, pl.ds(j * CW, CW)],
+            src_ref=up_from.at[:, pl.ds(j * CW, CW)],
             dst_ref=up.at[:, pl.ds(place(j, 0), CW)],
             send_sem=perm_send.at[j],
             recv_sem=perm_recv.at[j],
@@ -157,6 +167,7 @@
         pltpu.make_async_copy(whole, whole, sem).wait()
 
     mark("perm01")
+    up_loads[0].wait()
     for j in (0, 1):
         permute(j).start()
 
@@ -196,6 +207,7 @@
     mark("a2a_f1_send")
     exchange(own_f, got_f, a2a_sem.at[0], a2a_sem.at[1])
     exchange(totals, tot_in, tot_sem.at[0], tot_sem.at[1])
+    up_loads[1].wait()
     for j in (2, 3, 4):
         permute(j).start()
     q_load.wait()
@@ -267,7 +279,7 @@
         copy.wait()
 
     def hidden(start, depth, first):
-        @pl.loop(0, 4)
+        @pl.loop(0, 4, unroll=2)
         def _(n):
             at = pl.ds(pl.multiple_of(n * 512, 512), 512)
             part = nt(up[:, start : start + depth], w[at, start : start + depth])
@@ -285,10 +297,10 @@
         for j in chunks:
             forward(j).wait_recv()
 
-    @pl.loop(0, HEADS)
+    @pl.loop(0, HEADS, unroll=2)
     def _(h):
-        scale = jnp.broadcast_to(gain[:, lanes(h)], (HEAD, HEAD)).T
-        w_last[lanes(h), :] = (w[lanes(h), MODEL - CW :].astype(F32) * scale).astype(BF)
+        turned = w[lanes(h), MODEL - CW :].astype(F32).T
+        w_last[:, lanes(h)] = (turned * gain[:, lanes(h)]).astype(BF)
 
     mark("relay012")
     relay(0, 1, 2, 3)
@@ -362,7 +374,7 @@
     relayed(8, 9)
     mark("hidden89")
 
-    @pl.loop(0, 4)
+    @pl.loop(0, 4, unroll=2)
     def _(n):
         at = pl.ds(pl.multiple_of(n * 512, 512), 512)
         new = gh[:, at] + nt(up[:, 2048:2560], w[at, 2048:2560])
@@ -383,7 +395,7 @@
     relayed(10)
     mark("sib10own11")
 
-    @pl.loop(0, 4)
+    @pl.loop(0, 4, unroll=2)
     def _(n):
         at = pl.ds(pl.multiple_of(n * 512, 512), 512)
         new = gh[:, at] + nt(up[:, 2688:2944], w[at, 2688:2944])
@@ -423,33 +435,25 @@
         whole = ref.at[pl.ds(0, BLOCKS - 1), rows]
         pltpu.make_async_copy(whole, whole, a2a_sem.at[sem]).wait()
 
-    def last_step(n):
-        at = pl.ds(pl.multiple_of(zs[n] * 512, 512), 512)
-        gh[:, at] += nt(up_last, w_last[at, :])
-
-    def passing(n):
-        for j in range(4):
-            h = 4 * zs[n] + j
-            grad = (gh[:, lanes(h)] - fac[...] * att[:, lanes(h)]).astype(BF)
-            ga[:, lanes(h)] = grad
-            passed = nn(wqt[h], grad).astype(BF)
+    def passing(i):
+        at = pair_lanes(i)
+        both = gh[:, at] + nn(up_last, w_last[:, at])
+        factor = fac[...]
+        both = both - jnp.concatenate([factor, factor], axis=1) * att[:, at]
+        both = both.astype(BF)
+        ga[:, at] = both
+        for side in (0, 1):
+            h = 2 * i + side
+            passed = nn(wqt[h], both[:, side * HEAD : (side + 1) * HEAD]).astype(BF)
             own_b[2 * h] = passed[:ROWS]
             own_b[2 * h + 1] = passed[ROWS:]
 
-    def send_low(part):
-        for p, device in part:
+    for group in ((2, 1), (3, 0)):
+        for n in group:
+            passing(2 * zs[n])
+            passing(2 * zs[n] + 1)
+        for p, device in (peer(at) for at in offsets if at[0] in group):
             send_piece(own_b, got_b, p, device, low_rows, 4)
-
-    last_step(0)
-    last_step(1)
-    passing(0)
-    passing(1)
-    last_step(2)
-    last_step(3)
-    send_low(peers[:15])
-    passing(2)
-    passing(3)
-    send_low(peers[15:])
     mark("send_high")
     for p, device in peers:
         send_piece(own_b, got_b, p, device, high_rows, 6)
@@ -497,13 +501,13 @@
     mark("scan_ba")
     scan_back(low_rows)
     mark("grad2")
-    pl.loop(3, 5)(gradients)
+    pl.loop(3, 4)(gradients)
     mark("wait_b1b")
     piece_arrived(got_b, high_rows, 7)
     mark("scan_bb")
     scan_back(high_rows)
     mark("grad3")
-    pl.loop(5, HEADS // 2)(gradients)
+    pl.loop(4, HEADS // 2)(gradients)
     mark("wait_b2")
     piece_arrived(later, low_rows, 9)
     piece_arrived(later, high_rows, 11)
@@ -531,17 +535,16 @@
     def put(src, dst, at, i):
         pltpu.make_async_copy(src.at[:, at], dst.at[0, :, at], out_sem.at[i]).start()
 
-    @pl.loop(0, HEADS // 4)
-    def _(n):
-        for i in (2 * n, 2 * n + 1):
-            at = pair_lanes(i)
-            lt = two_states(later, i)
-            tail = two_columns(tails, i)
-            dks[:, at] = (att[:, at] + tail * nt(v[:, at], lt)).astype(BF)
-            dvs[:, at] = (gh[:, at] + tail * nn(k[:, at], lt)).astype(BF)
-        four = pl.ds(pl.multiple_of(n * 512, 512), 512)
-        put(dks, dk_hbm, four, 1)
-        put(dvs, dv_hbm, four, 2)
+    for i in range(HEADS // 2):
+        at = pair_lanes(i)
+        lt = two_states(later, i)
+        tail = two_columns(tails, i)
+        dks[:, at] = (att[:, at] + tail * nt(v[:, at], lt)).astype(BF)
+        dvs[:, at] = (gh[:, at] + tail * nn(k[:, at], lt)).astype(BF)
+        if i % 2 == 1:
+            part = pl.ds((i - 1) * 2 * HEAD, 4 * HEAD)
+            put(dks, dk_hbm, part, 1)
+            put(dvs, dv_hbm, part, 2)
 
     for i, (src, dst) in enumerate(((dqs, dq_hbm), (dks, dk_hbm), (dvs, dv_hbm))):
         pltpu.make_async_copy(src, dst.at[0], out_sem.at[i]).wait()
@@ -581,8 +584,9 @@
             vmem((HEADS, TOK), F32),
             vmem((TOK, 4 * CW), BF),
             vmem((TOK, 4 * CW), BF),
-            vmem((WIDTH, CW), BF),
-            dma((19,)),
+            vmem((CW, WIDTH), BF),
+            vmem((TOK, MODEL // 2), BF),
+            dma((21,)),
             dma((2,)),
             dma((12,)),
             dma((CHUNKS,)), dma((CHUNKS,)), dma((CHUNKS,)), dma((CHUNKS,)),

time: 80.3 us -> 77.9 us (0.970)
  Pallas kernels: 79.1 us -> 76.3 us
    pallas_call x1, Pallas kernels: 76.1 us -> 73.7 us  [local(): pl.pallas_call(kernel, out_shape=(rows_bf, rows_f32, rows_f32, rows_bf, r...]
where the time goes in v5:
time: 77.9 us; the launch traced here: 77.1 us
  Pallas kernels  76.3 us (98%)
  between operations  0.8 us (1%)
    pallas_call x1, Pallas kernels, local(): pl.pallas_call(kernel, out_shape=(rows_bf, rows_f32, rows_f32, rows_bf, r...  73.7 us
    pallas_call x1, Pallas kernels, local(): pl.pallas_call(finish, out_shape=(out, out, out), in_specs=[here] * 7, ou...  2.67 us

profile of v5, /device:TPU:1, one launch (start us, length us, event | category | flops | bytes accessed | tf_op | source)
XLA Modules:
  0.0 77.1 jit_solution(760375250468967696)
XLA Ops:
  0.6 73.7 %decayed_backward.1 = (bf16[512,2048]{1,0:T(8,128)(2,1)S(1)}, f32[512,2048]{1,0:T(8,128)S(1)}, f32[512,2048]{1,0:T(8,128)S(1)}, bf16[512,2048]{1,0:T(8,128)(2,1)...) custom-call(bf16[1,512,2048]{2,1,0:T(8,128)(2,1)} %q_hbm.1, ...), custom_call_target="tpu_custom_call" | custom-call | tf_op jit(solution)/shard_map/decayed_backward/pallas_call | solution.py:564
  74.3 2.7 %finish.1 = (bf16[1,512,2048]{2,1,0:T(8,128)(2,1)}, bf16[1,512,2048]{2,1,0:T(8,128)(2,1)}, bf16[1,512,2048]{2,1,0:T(8,128)(2,1)}) custom-call(bf16[512,2048]{1,0:T(8,128)(2,1)S(1)} %get-tuple-element.10.dqs, f32[512,2048]{1,0:T(8,128)S(1)} %get-tuple-element.11.att, f32[512,2048]{1,0:T(8,128)S(1)} %get-tuple-element.12.gh, ...), custom_call_target="tpu_custom_call" | custom-call | tf_op jit(solution)/shard_map/finish/pallas_call | solution.py:602

commit v6 on v5

--- a/solution.py
+++ b/solution.py
@@ -475,13 +475,8 @@
             more = inter[:, side * HEAD : (side + 1) * HEAD]
             dqs[:HALF, lanes(h)] = (dq0 + more[:HALF]).astype(BF)
             dqs[HALF:, lanes(h)] = (dq1 + more[HALF:]).astype(BF)
-            t00, t01, t11 = turned_parts(h)
-            n0 = jnp.concatenate(
-                [(nt(v0, g0) * t00).astype(BF), (nt(v0, g1) * t01).astype(BF)], axis=1
-            )
-            n1 = (nt(v1, g1) * t11).astype(BF)
-            att[:HALF, lanes(h)] = nn(n0, qh)
-            att[HALF:, lanes(h)] = nn(n1, qh[HALF:])
+            att[:HALF, lanes(h)] = nn(jnp.concatenate([m00.T, m10.T], axis=1), qh)
+            att[HALF:, lanes(h)] = nn(m11.T, qh[HALF:])
             gh[:HALF, lanes(h)] = nn(mta[h], gah)
             gh[HALF:, lanes(h)] = nn(mtb[h], g1)
 

time: 77.9 us -> 78 us (level)
  no operation moved by 1% of the time
where the time goes in v6:
time: 78 us; the launch traced here: 77.1 us
  Pallas kernels  76.3 us (98%)
  between operations  0.8 us (1%)
    pallas_call x1, Pallas kernels, local(): pl.pallas_call(kernel, out_shape=(rows_bf, rows_f32, rows_f32, rows_bf, r...  73.6 us
    pallas_call x1, Pallas kernels, local(): pl.pallas_call(finish, out_shape=(out, out, out), in_specs=[here] * 7, ou...  2.67 us

profile of v6, /device:TPU:1, one launch (start us, length us, event | category | flops | bytes accessed | tf_op | source)
XLA Modules:
  0.0 77.1 jit_solution(2360035099238064216)
XLA Ops:
  0.6 73.6 %decayed_backward.1 = (bf16[512,2048]{1,0:T(8,128)(2,1)S(1)}, f32[512,2048]{1,0:T(8,128)S(1)}, f32[512,2048]{1,0:T(8,128)S(1)}, bf16[512,2048]{1,0:T(8,128)(2,1)...) custom-call(bf16[1,512,2048]{2,1,0:T(8,128)(2,1)} %q_hbm.1, ...), custom_call_target="tpu_custom_call" | custom-call | tf_op jit(solution)/shard_map/decayed_backward/pallas_call | solution.py:559
  74.3 2.7 %finish.1 = (bf16[1,512,2048]{2,1,0:T(8,128)(2,1)}, bf16[1,512,2048]{2,1,0:T(8,128)(2,1)}, bf16[1,512,2048]{2,1,0:T(8,128)(2,1)}) custom-call(bf16[512,2048]{1,0:T(8,128)(2,1)S(1)} %get-tuple-element.10.dqs, f32[512,2048]{1,0:T(8,128)S(1)} %get-tuple-element.11.att, f32[512,2048]{1,0:T(8,128)S(1)} %get-tuple-element.12.gh, ...), custom_call_target="tpu_custom_call" | custom-call | tf_op jit(solution)/shard_map/finish/pallas_call | solution.py:597
